TPU v7x, 32 devices: a whole 2x2x4 slice. The times are simulated.
32 devices in a mesh: sub: 8 (over z, x), rng: 4 (over y, core).
Axes of the slice: x: 2, y: 2, z: 4, core: 2. Of those that a mesh axis runs over, the one named last changes fastest.
Arguments:
- echoes: bfloat16 [2, 4, 1024, 2048], P(None, None, 'sub', 'rng'), may hold values from -6 to 6
- steering: bfloat16 [2, 256, 256], replicated, may hold values from -0.25 to 0.25
- sub_map: int32 [8], replicated, may hold values from 0 to 7, each once
- band_offset: int32 [8, 3, 2, 256], P('sub'), may hold values from 0 to 248, as said below
- interp_weight: bfloat16 [8, 3, 2, 8, 256], P('sub'), may hold values from -1.5 to 1.5
- range_frac: float32 [8, 3, 2, 256], P('sub'), may hold values from 0 to 1
- phase_rate: float32 [8, 3, 2, 256], P('sub'), may hold values from -40 to 40
Outputs:
- image: bfloat16 [2, 4096, 2048], P(None, 'rng', 'sub')
Inputs may be any that keep to these rules, and one draw needn't show every extreme that they name: `sub_map`: each number appears once. `band_offset`: an entry for section i and segment s lies in h * 128 to (h + 1) * 128 - 8, where h is bit s of i.
All inputs are finite; a program needn't handle non-finite values.
Results may differ from a plain program's by a relative error of at most 0.0062.
Values may be sent and summed in bfloat16 or wider, within the bound.
No kernel may reach another device: no remote copies, remote signals or barrier semaphores. Data moves between devices by JAX's collectives and lax.ppermute only.
A program may use at most 64 MiB of HBM per device.

v0:
```python
import functools

import jax
import jax.numpy as jnp
from jax import lax
from jax.experimental import pallas as pl
from jax.experimental.pallas import tpu as pltpu
from jax.sharding import PartitionSpec as P


HALO = 8
KINDS = 6
MIB = 1 << 20
WHOLE = pl.BlockSpec(memory_space=pltpu.VMEM)
SCALARS = pl.BlockSpec(memory_space=pltpu.SMEM)
FAR = pl.BlockSpec(memory_space=pltpu.HBM)


def exchanged(block, axis, mask):
    count = lax.axis_size(axis)
    return lax.ppermute(block, axis, [(source, source ^ mask) for source in range(count)])


def params(mib):
    return pltpu.CompilerParams(vmem_limit_bytes=mib * MIB)


def cost(flops):
    return pl.CostEstimate(flops=flops, bytes_accessed=MIB, transcendentals=0)


def product(left, right):
    return (
        left[0] * right[0] - left[1] * right[1],
        left[0] * right[1] + left[1] * right[0],
    )


def pack_rows(terms, taps):
    return -(-(terms * (taps + KINDS)) // 8) * 8


def cut_kernel(slabs, segments, taps, half, echoes, offset, weight, fraction, rate, *refs):
    slices, packs = refs[:slabs], refs[slabs : slabs + 2]
    held, semaphores, small = refs[slabs + 2 : slabs + 6], refs[slabs + 6], refs[slabs + 7]
    group = 1 << segments
    member = lax.axis_index("sub") & (group - 1)
    slab = lax.axis_index("rng")
    loads = [
        pltpu.make_async_copy(source, target, small.at[index])
        for index, (source, target) in enumerate(zip((offset, weight, fraction, rate), held))
    ]
    copies = []
    for mask in range(slabs - 1, -1, -1):
        for c in range(2):
            copies.append(
                pltpu.make_async_copy(
                    echoes.at[c, slab ^ mask], slices[mask].at[c], semaphores.at[mask, c]
                )
            )
    for copy in loads + copies:
        copy.start()
    for copy in loads:
        copy.wait()
    offset, weight, fraction, rate = held
    angles = weight.shape[-1]
    for pack, chosen in ((packs[0], range(segments - 1)), (packs[1], (segments - 1,))):
        kinds = [[] for _ in range(KINDS)]
        terms = 2 * len(chosen)
        for index, segment in enumerate(chosen):
            base = ((member >> segment) & 1) * half
            kinds[0].append((offset[0, segment] - base).astype(jnp.float32))
            slot = 1
            for source, count in ((fraction, 2), (rate, 3)):
                rest = source[0, segment]
                for _ in range(count):
                    part = rest.astype(jnp.bfloat16).astype(jnp.float32)
                    kinds[slot].append(part)
                    rest = rest - part
                    slot += 1
            for child in range(2):
                term = index * 2 + child
                pack[term * taps : (term + 1) * taps, :] = weight[0, segment, child]
        rows = [piece for kind in kinds for piece in kind]
        padding = pack_rows(terms, taps) - terms * (taps + KINDS)
        if padding:
            rows.append(jnp.zeros((padding, angles), jnp.float32))
        pack[terms * taps :, :] = jnp.concatenate(rows, axis=0).astype(jnp.bfloat16)
    for copy in copies:
        copy.wait()


def table_kernel(members, terms, masks, taps, half, rows, lines, range_rows, total_range, *refs):
    steps = len(masks[0]) if masks else 0
    own, mine, theirs = refs[0], refs[1 : 1 + steps], refs[1 + steps : 1 + 2 * steps]
    bands, waves, weights, raw, dense = refs[1 + 2 * steps :]
    angles = bands.shape[-1]
    member = lax.axis_index("sub") & (members - 1)
    slab = lax.axis_index("rng")

    def fill(piece, section):
        values = piece[...].astype(jnp.float32)
        for term in range(terms):
            weights[section, term] = values[term * taps : (term + 1) * taps]
        start = terms * taps
        kind = [values[start + k * terms : start + (k + 1) * terms] for k in range(KINDS)]
        raw[section, 0] = kind[0]
        raw[section, 1] = kind[1] + kind[2]
        raw[section, 2] = kind[3] + kind[4] + kind[5]

    if masks:
        core = slab & 1
        fill(own, member)
        for side, received in ((0, mine), (1, theirs)):
            holder = core if side == 0 else 1 - core
            for step in range(steps):
                pair = [masks[c][step] if step < len(masks[c]) else 0 for c in range(2)]
                mask = jnp.where(holder == 0, pair[0], pair[1])

                @pl.when(mask != 0)
                def _(step=step, received=received, mask=mask):
                    fill(received[step], member ^ mask)

        first_row, row_step = slab * range_rows + member * rows, 0
    else:
        for section in range(members):
            fill(own, section)
        first_row, row_step = slab * range_rows, rows

    for start in range(0, members * terms, 8):
        place = slice(start, start + 8)
        sections = range(start // terms, (start + 8) // terms)

        def keep(kind, value):
            for part in range(angles // 128):
                dense[kind, part, place] = value[:, part * 128 : (part + 1) * 128]

        given = [
            jnp.concatenate([raw[section, kind] for section in sections], axis=0)
            for kind in range(3)
        ]
        keep(0, given[0])
        keep(1, given[1])
        rate = given[2]
        number = start + lax.broadcasted_iota(jnp.int32, (8, angles), 0)
        first = first_row + (number // terms) * row_step
        angle = first.astype(jnp.float32) / float(total_range) * rate
        keep(3, jnp.cos(angle))
        keep(4, jnp.sin(angle))
        angle = rate / float(total_range)
        turn = jnp.cos(angle), jnp.sin(angle)
        for power in range(5):
            keep(5 + 2 * power, turn[0])
            keep(6 + 2 * power, turn[1])
            turn = product(turn, turn)

    sub_rows = lax.broadcasted_iota(jnp.int32, (8, 128), 0)

    def entry(index, carry):
        section, term = index // terms, index % terms
        for part in range(angles // 128):
            lanes = pl.ds(part * 128, 128)

            def row(kind):
                return dense[kind, part, pl.ds(index, 1), :]

            def bands_of():
                weight = weights[section, term, :, lanes]
                offset = row(0).astype(jnp.int32)
                fraction = row(1)
                tap = sub_rows - offset
                block_of = -(tap >> 3)
                picked = jnp.take_along_axis(weight, tap & 7, axis=0)
                near, far = picked * (1.0 - fraction), picked * fraction
                for block in range(half // 16):
                    hits = [block_of == 2 * block + step for step in range(2)]
                    for source, base in ((near, 0), (far, half)):
                        pair = [jnp.where(hit, source, 0.0) for hit in hits]
                        place = slice(base + block * 16, base + (block + 1) * 16)
                        bands[section, term, place, lanes] = jnp.concatenate(pair, axis=0).astype(
                            jnp.bfloat16
                        )

            if masks:
                bands_of()
            else:
                pl.when(section == 0)(bands_of)
            wave = tuple(jnp.broadcast_to(row(3 + c), (8, 128)) for c in range(2))
            for power in range(3):
                chosen = (sub_rows >> power) & 1 == 1
                wave = product(
                    wave,
                    (
                        jnp.where(chosen, row(5 + 2 * power), 1.0),
                        jnp.where(chosen, row(6 + 2 * power), 0.0),
                    ),
                )
            eight, sixteen = (row(11), row(12)), (row(13), row(14))
            chain = [wave, product(wave, eight)]
            for block in range(lines // 8):
                wave = chain[block % 2]
                for c in range(2):
                    waves[section, term, c, block * 8 : (block + 1) * 8, lanes] = wave[c]
                chain[block % 2] = product(wave, sixteen)
        return carry

    lax.fori_loop(0, members * terms, entry, 0)


def formed(steering, re_part, im_part):
    def dot(left, right):
        return lax.dot_general(
            left, right, (((1,), (1,)), ((), ())), preferred_element_type=jnp.float32
        )

    real_weight, imag_weight = steering[0], steering[1]
    return (
        dot(re_part, real_weight) + dot(im_part, -imag_weight),
        dot(re_part, imag_weight) + dot(im_part, real_weight),
    )


def place_of(sub_map, group, slabs, slab, index):
    if slabs == 1:
        return index
    per_slab = group // slabs
    block = (slab ^ (index // per_slab)) * per_slab + index % per_slab
    place = 0
    for section in range(group):
        place = jnp.where(sub_map[section] == block, section, place)
    return place


def form_kernel(group, pulse_count, sources, sub_map, *refs):
    blocks, steering, image = refs[:sources], refs[sources], refs[sources + 1]
    half = image.shape[-1]
    per_source = group // sources
    slab = lax.axis_index("rng")
    for source in range(sources):
        for piece in range(per_source):
            columns = slice(piece * pulse_count, (piece + 1) * pulse_count)
            target = place_of(sub_map, group, sources, slab, source * per_source + piece)
            parts = [blocks[source][c, :, columns] for c in range(2)]
            for c, value in enumerate(formed(steering, *parts)):
                for window in range(2):
                    image[target, c, window] = value[:, window * half : (window + 1) * half]


def turned(values, block):
    total = None
    for value, wave in values:
        part = value[block * 16 : block * 16 + 8], value[block * 16 + 8 : block * 16 + 16]
        turn = tuple(wave[c, block * 8 : block * 8 + 8] for c in range(2))
        term = product(turn, part)
        total = term if total is None else (total[0] + term[0], total[1] + term[1])
    return total


def contracted(rows_of, lines, matrix):
    pieces = []
    for block in range(lines // 8):
        sides = []
        for start in (block * 8, block * 8 + 1):
            both = [rows_of(c, start) for c in range(2)]
            sides.append(jnp.concatenate(both, axis=0).astype(jnp.bfloat16))
        pieces.append(jnp.concatenate(sides, axis=1))
    return jnp.dot(jnp.concatenate(pieces, axis=0), matrix, preferred_element_type=jnp.float32)


def merge_kernel(group, segments, rows, pulse_count, sources, sub_map, *refs):
    image, edge, steering, bands, waves = refs[:5]
    outs, edges = refs[5 : 5 + group], refs[5 + group]
    stores = refs[6 + group :]
    half = image.shape[-1]
    member = lax.axis_index("sub") & (group - 1)
    per_source = group // sources
    below = lax.axis_index("rng")
    if sources > 1:
        below = jnp.minimum(below + jnp.where(member == group - 1, 1, 0), sources - 1)

    edge_parts = [[], []]
    for source in range(sources):
        for piece in range(per_source):
            columns = slice(piece * pulse_count, (piece + 1) * pulse_count)
            for c in range(2):
                edge_parts[c].append(edge[source, c, :, columns])
    values = formed(steering, *[jnp.concatenate(parts, axis=0) for parts in edge_parts])
    for index in range(group):
        target = place_of(sub_map, group, sources, below, index)
        for c in range(2):
            value = values[c][index * HALO : (index + 1) * HALO]
            for window in range(2):
                edges[target, c, window, 0:HALO] = value[:, window * half : (window + 1) * half]
                edges[target, c, window, HALO:] = jnp.zeros((8, half), jnp.float32)

    def rows_of(segment, section, window, c, start):
        if segment > 0:
            return stores[segment - 1][section, c, window, start : start + 8]
        if start + 8 <= rows:
            return image[section, c, window, start : start + 8]
        if start >= rows:
            return edges[section, c, window, start - rows : start - rows + 8]
        return jnp.concatenate(
            [
                image[section, c, window, start:rows],
                edges[section, c, window, 0 : start + 8 - rows],
            ],
            axis=0,
        )

    for segment in range(segments - 1):

        def step(section, carry, segment=segment):
            low = section & ~(1 << segment)
            window = (section >> segment) & 1
            values = []
            for child in range(2):
                source, term = low | (child << segment), segment * 2 + child
                reader = functools.partial(rows_of, segment, source, window)
                value = contracted(reader, rows + 8, bands[section, term])
                values.append((value, waves.at[section, term]))
            for block in range(rows // 8 + 1):
                for c, total in enumerate(turned(values, block)):
                    for side in range(2):
                        stores[segment][section, c, side, block * 8 : block * 8 + 8] = total[
                            :, side * half : (side + 1) * half
                        ]
            for c in range(2):
                for side in range(2):
                    stores[segment][section, c, side, rows + 8 :] = jnp.zeros(
                        (8, half), jnp.float32
                    )
            return carry

        lax.fori_loop(0, group, step, 0, unroll=4)

    last = stores[segments - 2]
    for mask in range(group):
        section = member ^ mask
        low = section & ~(1 << (segments - 1))
        window = (section >> (segments - 1)) & 1
        extra = []
        for child in range(2):
            for c in range(2):
                start = (child * 2 + c) * rows
                source = last.at[low | (child << (segments - 1)), c, window]
                outs[mask][start : start + rows] = source[0:rows].astype(jnp.bfloat16)
                extra.append(source[rows : rows + 1])
        extra.append(jnp.zeros((4, half), jnp.float32))
        outs[mask][4 * rows :] = jnp.concatenate(extra, axis=0).astype(jnp.bfloat16)


def final_kernel(masks, group, rows, first, *refs):
    count = len(masks)
    parts, (bands, waves) = refs[:count], refs[count : count + 2]
    result, store, mine, semaphores = refs[count + (2 if first else 3) :]
    half = store.shape[-1]
    member = lax.axis_index("sub") & (group - 1)
    copies = []
    for index, mask in enumerate(masks):
        part = parts[index]
        extra = part[4 * rows :].astype(jnp.float32)
        for side in range(4):
            store[index, side, 0:rows] = part[side * rows : (side + 1) * rows].astype(jnp.float32)
            store[index, side, rows:] = jnp.broadcast_to(extra[side : side + 1], (8, half))
        values = []
        for child in range(2):

            def rows_of(c, start, index=index, child=child):
                return store[index, child * 2 + c, start : start + 8]

            value = contracted(rows_of, rows, bands[0, child])
            values.append((value, waves.at[member ^ mask, child]))
        held = None
        for block in range(rows // 8):
            totals = turned(values, block)
            if block % 2 == 0:
                held = totals
                continue
            for c in range(2):
                mine[index, c, block * 8 - 8 : block * 8 + 8] = jnp.concatenate(
                    [held[c], totals[c]], axis=0
                ).astype(jnp.bfloat16)
        start = pl.multiple_of((member ^ mask) * rows, rows)
        for c in range(2):
            copy = pltpu.make_async_copy(
                mine.at[index, c], result.at[c, pl.ds(start, rows)], semaphores.at[index, c]
            )
            copy.start()
            copies.append(copy)
    for copy in copies:
        copy.wait()


def send_order(group):
    masks = list(range(1, group))
    far = sorted([mask for mask in masks if mask >= group // 2], reverse=True)
    near = sorted([mask for mask in masks if mask < group // 2], reverse=True)
    return far[:2] + near + far[2:]


def on_device(echoes, steering, sub_map, band_offset, interp_weight, range_frac, phase_rate):
    slabs = lax.axis_size("rng")
    subs = lax.axis_size("sub")
    segments, taps = interp_weight.shape[1], interp_weight.shape[3]
    group = 1 << segments
    groups = subs // group
    angles, pulse_count = steering.shape[1], steering.shape[2]
    half = angles // 2
    slab = lax.axis_index("rng")
    range_rows = echoes.shape[2] * subs
    rows = range_rows // group
    early, late = 2 * (segments - 1), 2

    cut = (2,) + echoes.shape[2:]
    tables_in = (band_offset, interp_weight, range_frac, phase_rate)
    *quarters, early_pack, late_pack = pl.pallas_call(
        functools.partial(cut_kernel, slabs, segments, taps, half),
        out_shape=[jax.ShapeDtypeStruct(cut, jnp.bfloat16)] * slabs
        + [
            jax.ShapeDtypeStruct((pack_rows(terms, taps), angles), jnp.bfloat16)
            for terms in (early, late)
        ],
        in_specs=[FAR] * 5,
        out_specs=[WHOLE] * (slabs + 2),
        scratch_shapes=[pltpu.VMEM(value.shape, value.dtype) for value in tables_in]
        + [pltpu.SemaphoreType.DMA((slabs, 2)), pltpu.SemaphoreType.DMA((4,))],
        compiler_params=params(60),
        cost_estimate=cost(1_000_000_000),
        name="cut",
    )(echoes, *tables_in)

    received = [quarters[0]] + [None] * (slabs - 1)
    for mask in range(slabs - 1, 0, -1):
        received[mask] = exchanged(quarters[mask], "rng", mask)

    masks = list(range(group - 1, 0, -1))
    masks = (masks[0::2], masks[1::2])
    mine, theirs = [], []
    for step in range(len(masks[0])):
        route = []
        for s in range(subs):
            for q in range(slabs):
                if step < len(masks[q & 1]):
                    route.append((s * slabs + q, (s ^ masks[q & 1][step]) * slabs + q))
        mine.append(lax.ppermute(early_pack, ("sub", "rng"), route))
    for piece in mine:
        theirs.append(exchanged(piece, "rng", 1))

    if groups == 1:
        blocks = received
    else:
        ordered = jnp.zeros((slabs,) + received[0].shape, received[0].dtype)
        for mask, block in enumerate(received):
            ordered = lax.dynamic_update_index_in_dim(ordered, block, slab ^ mask, 0)
        every = jnp.moveaxis(ordered, 0, 2).reshape(2, -1, subs, pulse_count)
        every = jnp.take(every, sub_map, axis=2)
        every = lax.ppermute(
            every,
            "sub",
            [(old, (old % groups) * group + old // groups) for old in range(subs)],
        ).reshape(2, -1, groups, group * pulse_count)
        lanes = [[g * group + m for g in range(groups)] for m in range(group)]
        every = lax.all_to_all(every, "sub", 2, 1, axis_index_groups=lanes, tiled=True)
        blocks = [every.reshape(2, rows, group * pulse_count)]

    edge_rows = jnp.stack([block[:, :HALO] for block in blocks])
    route = []
    for number in range(subs):
        for q in range(slabs):
            if number % group > 0:
                route.append((number * slabs + q, (number - 1) * slabs + q))
            elif q > 0:
                route.append((number * slabs + q, (number + group - 1) * slabs + q - 1))
    edge = lax.ppermute(edge_rows, ("sub", "rng"), route)

    def tables(terms, sources, held, lines, arrays):
        return pl.pallas_call(
            functools.partial(
                table_kernel,
                group,
                terms,
                sources,
                taps,
                half,
                rows,
                lines,
                range_rows,
                slabs * range_rows,
            ),
            out_shape=(
                jax.ShapeDtypeStruct((held, terms, angles, angles), jnp.bfloat16),
                jax.ShapeDtypeStruct((group, terms, 2, lines, angles), jnp.float32),
            ),
            in_specs=[WHOLE] * len(arrays),
            out_specs=(WHOLE, WHOLE),
            scratch_shapes=[
                pltpu.VMEM((group, terms, taps, angles), jnp.float32),
                pltpu.VMEM((group, 3, terms, angles), jnp.float32),
                pltpu.VMEM((15, angles // 128, group * terms, 128), jnp.float32),
            ],
            compiler_params=params(4),
            cost_estimate=cost(2_000_000_000),
        )(*arrays)

    bands, waves = tables(early, masks, group, rows + 8, [early_pack, *mine, *theirs])

    image = pl.pallas_call(
        functools.partial(form_kernel, group, pulse_count, len(blocks)),
        out_shape=jax.ShapeDtypeStruct((group, 2, 2, rows, half), jnp.float32),
        in_specs=[SCALARS] + [WHOLE] * (len(blocks) + 1),
        out_specs=WHOLE,
        compiler_params=params(8),
        cost_estimate=cost(1_000_000_000),
        name="form",
    )(sub_map, *blocks, steering)

    sent = pl.pallas_call(
        functools.partial(merge_kernel, group, segments, rows, pulse_count, len(blocks)),
        out_shape=[jax.ShapeDtypeStruct((4 * rows + 8, half), jnp.bfloat16)] * group,
        in_specs=[SCALARS] + [WHOLE] * 5,
        out_specs=[WHOLE] * group,
        scratch_shapes=[pltpu.VMEM((group, 2, 2, 16, half), jnp.float32)]
        + [pltpu.VMEM((group, 2, 2, rows + 16, half), jnp.float32)] * (segments - 1),
        compiler_params=params(12),
        cost_estimate=cost(4_000_000_000),
        name="merge",
    )(sub_map, image, edge, steering, bands, waves)

    order = send_order(group)
    arrived = {0: sent[0]}
    for mask in order:
        arrived[mask] = exchanged(sent[mask], "sub", mask)
    last_bands, last_waves = tables(late, None, 1, rows, [late_pack])
    result = None
    turns = [[0] + order[:1] + order[2:-2], order[1:2], order[-2:-1], order[-1:]]
    for chosen in turns:
        count = len(chosen)
        shape = jax.ShapeDtypeStruct((2, range_rows, angles), jnp.bfloat16)
        previous = [] if result is None else [result]
        result = pl.pallas_call(
            functools.partial(final_kernel, chosen, group, rows, result is None),
            out_shape=shape,
            in_specs=[WHOLE] * (count + 2) + [FAR] * len(previous),
            out_specs=FAR,
            scratch_shapes=[
                pltpu.VMEM((count, 4, rows + 8, half), jnp.float32),
                pltpu.VMEM((count, 2, rows, angles), jnp.bfloat16),
                pltpu.SemaphoreType.DMA((count, 2)),
            ],
            input_output_aliases={count + 2: 0} if previous else {},
            compiler_params=params(6),
            cost_estimate=cost(1_000_000_000),
            name="final",
        )(*[arrived[mask] for mask in chosen], last_bands, last_waves, *previous)
    return result


def solution(mesh):
    in_specs = (
        P(None, None, "sub", "rng"),
        P(),
        P(),
        P("sub", None, None, None),
        P("sub", None, None, None, None),
        P("sub", None, None, None),
        P("sub", None, None, None),
    )
    return jax.shard_map(
        on_device, mesh=mesh, in_specs=in_specs, out_specs=P(None, "rng", "sub"), check_vma=False
    )
```

profile of v0, /device:TPU:0, one launch (start us, length us, event | category | flops | bytes accessed | tf_op | source)
XLA Modules:
  0.0 65.9 jit_solution(1241203557149114435)
XLA Ops:
  0.0 2.4 %cut.1 = (bf16[2,128,512]{2,1,0:T(8,128)(2,1)}, bf16[2,128,512]{2,1,0:T(8,128)(2,1)}, bf16[2,128,512]{2,1,0:T(8,128)(2,1)}, bf16[2,128,512]{2,1,0:T(8,128)(2,1)}...) custom-call(bf16[2,4,128,512]{3,2,1,0:T(8,128)(2,1)} %echoes.1, s32[1,3,2,256]{3,2,1,0:T(2,128)} %offset.1, ...), custom_call_target="tpu_custom_call" | custom-call | flops 1000000000 | bytes 1048576 | tf_op jit(solution)/shard_map/cut/pallas_call | solution.py:417
  2.4 4.0 %collective-permute-start.6 = (bf16[56,256]{1,0:T(8,128)(2,1)}, bf16[56,256]{1,0:T(8,128)(2,1)S(1)}, u32[]{:S(2)}, u32[]{:S(2)}) collective-permute-start(bf16[56,256]{1,0:T(8,128)(2,1)} %get-tuple-element.27.refs_0_), channel_id=1, source_target_pairs={{0,12},{1,9},{2,14},{3,11},{4,8},{5,13},{6,10},{7,15},{8,4},{9,1},... | collective-permute-start | bytes 86024 | tf_op jit(solution)/shard_map/ppermute | solution.py:446
  6.5 2.4 %collective-permute-start.7 = (bf16[56,256]{1,0:T(8,128)(2,1)}, bf16[56,256]{1,0:T(8,128)(2,1)S(1)}, u32[]{:S(2)}, u32[]{:S(2)}) collective-permute-start(bf16[56,256]{1,0:T(8,128)(2,1)} %get-tuple-element.27.refs_0_), channel_id=1, source_target_pairs={{0,4},{2,6},{4,0},{6,2},{8,12},{10,14},{12,8},{14,10},{16,20},{18,... | collective-permute-start | bytes 86024 | tf_op jit(solution)/shard_map/ppermute | solution.py:446
  8.9 3.5 %collective-permute-start.4 = (bf16[56,256]{1,0:T(8,128)(2,1)}, bf16[56,256]{1,0:T(8,128)(2,1)S(1)}, u32[]{:S(2)}, u32[]{:S(2)}) collective-permute-start(bf16[56,256]{1,0:T(8,128)(2,1)} %get-tuple-element.27.refs_0_), channel_id=1, source_target_pairs={{0,28},{1,25},{2,30},{3,27},{4,24},{5,29},{6,26},{7,31},{8,20},{9,... | collective-permute-start | bytes 86024 | tf_op jit(solution)/shard_map/ppermute | solution.py:446
  12.6 1.6 %collective-permute-start.10 = (bf16[56,256]{1,0:T(8,128)(2,1)S(1)}, bf16[56,256]{1,0:T(8,128)(2,1)S(1)}, u32[]{:S(2)}, u32[]{:S(2)}) collective-permute-start(bf16[56,256]{1,0:T(8,128)(2,1)S(1)} %collective-permute-done.6.refs_3_), channel_id=1, source_target_pairs={{0,1},{1,0},{2,3},{3,2},{4,5},{5,4},{6,7},{7,6},{8,9},{9,8},{10,11... | collective-permute-start | bytes 86024 | tf_op jit(solution)/shard_map/ppermute | solution.py:21
  14.3 1.5 %collective-permute-done.4.refs_1_ = bf16[56,256]{1,0:T(8,128)(2,1)S(1)} collective-permute-done((bf16[56,256]{1,0:T(8,128)(2,1)}, bf16[56,256]{1,0:T(8,128)(2,1)S(1)}, u32[]{:S(2)}, u32[]{:S(2)}) %collective-permute-start.4) | collective-permute-done | bytes 28704 | tf_op jit(solution)/shard_map/ppermute | solution.py:446
  15.8 2.8 %collective-permute-done.5.refs_2_ = bf16[56,256]{1,0:T(8,128)(2,1)S(1)} collective-permute-done((bf16[56,256]{1,0:T(8,128)(2,1)}, bf16[56,256]{1,0:T(8,128)(2,1)S(1)}, u32[]{:S(2)}, u32[]{:S(2)}) %collective-permute-start.5) | collective-permute-done | bytes 28704 | tf_op jit(solution)/shard_map/ppermute | solution.py:446
  19.3 1.5 %collective-permute-start.1 = (bf16[2,128,512]{2,1,0:T(8,128)(2,1)}, bf16[2,128,512]{2,1,0:T(8,128)(2,1)S(1)}, u32[]{:S(2)}, u32[]{:S(2)}) collective-permute-start(bf16[2,128,512]{2,1,0:T(8,128)(2,1)} %get-tuple-element.25), channel_id=1, source_target_pairs={{0,2},{1,3},{2,0},{3,1},{4,6},{5,7},{6,4},{7,5},{8,10},{9,11},{10,... | collective-permute-start | bytes 786440 | tf_op jit(solution)/shard_map/ppermute | solution.py:21
  21.8 2.7 %shard_map.73 = (bf16[8,4,256,256]{3,2,1,0:T(8,128)(2,1)S(1)}, f32[8,4,2,136,256]{4,3,2,1,0:T(8,128)S(1)}) custom-call(bf16[56,256]{1,0:T(8,128)(2,1)S(1)} %copy-done.3, bf16[56,256]{1,0:T(8,128)(2,1)S(1)} %collective-permute-done.4.refs_1_, bf16[56,256]{1,0:T(8,128)(2,1)S(1)} %collective-permute-done.5.refs_2_, ...), custom_call_target="tpu_custom_call" | custom-call | flops 2000000000 | bytes 1048576 | tf_op jit(solution)/shard_map/pallas_call | solution.py:478
  24.6 3.7 %collective-permute-done.1.refs_2_ = bf16[2,128,512]{2,1,0:T(8,128)(2,1)S(1)} collective-permute-done((bf16[2,128,512]{2,1,0:T(8,128)(2,1)}, bf16[2,128,512]{2,1,0:T(8,128)(2,1)S(1)}, u32[]{:S(2)}, u32[]{:S(2)}) %collective-permute-start.1) | collective-permute-done | bytes 262176 | tf_op jit(solution)/shard_map/ppermute | solution.py:21
  28.3 1.3 %collective-permute-start.3 = (bf16[4,2,8,512]{3,2,1,0:T(8,128)(2,1)S(1)}, bf16[4,2,8,512]{3,2,1,0:T(8,128)(2,1)S(1)}, u32[]{:S(2)}, u32[]{:S(2)}) collective-permute-start(bf16[4,2,8,512]{3,2,1,0:T(8,128)(2,1)S(1)} %pad_maximum_fusion), channel_id=1, source_target_pairs={{1,28},{2,29},{3,30},{4,0},{5,1},{6,2},{7,3},{8,4},{9,5},{10,6},{1... | collective-permute-start | bytes 196616 | tf_op jit(solution)/shard_map/ppermute | solution.py:475
  29.6 2.0 %form.1.refs_0_ = f32[8,2,2,128,128]{4,3,2,1,0:T(8,128)S(1)} custom-call(s32[8]{0:T(128)S(1)} %copy-done.2, bf16[2,128,512]{2,1,0:T(8,128)(2,1)S(1)} %copy-done.1, bf16[2,128,512]{2,1,0:T(8,128)(2,1)S(1)} %collective-permute-done.refs_1_, bf16[2,128,512]{2,1,0:T(8,128)(2,1)S(1)} %collective-permute-done.1.refs_2_, ...), custom_call_target="tpu_custom_call" | custom-call | flops 1000000000 | bytes 1048576 | tf_op jit(solution)/shard_map/form/pallas_call | solution.py:508
  31.6 2.8 %collective-permute-done.3.refs_1_ = bf16[4,2,8,512]{3,2,1,0:T(8,128)(2,1)S(1)} collective-permute-done((bf16[4,2,8,512]{3,2,1,0:T(8,128)(2,1)S(1)}, bf16[4,2,8,512]{3,2,1,0:T(8,128)(2,1)S(1)}, u32[]{:S(2)}, u32[]{:S(2)}) %collective-permute-start.3) | collective-permute-done | bytes 65568 | tf_op jit(solution)/shard_map/ppermute | solution.py:475
  34.4 3.1 %merge.1 = (bf16[520,128]{1,0:T(8,128)(2,1)S(1)}, bf16[520,128]{1,0:T(8,128)(2,1)S(1)}, bf16[520,128]{1,0:T(8,128)(2,1)S(1)}, bf16[520,128]{1,0:T(8,128)(2,1)S(1...) custom-call(s32[8]{0:T(128)S(1)} %copy-done.2, ...), custom_call_target="tpu_custom_call" | custom-call | flops 4000000000 | bytes 1048576 | tf_op jit(solution)/shard_map/merge/pallas_call | solution.py:518
  37.5 4.7 %collective-permute-start.15 = (bf16[520,128]{1,0:T(8,128)(2,1)S(1)}, bf16[520,128]{1,0:T(8,128)(2,1)S(1)}, u32[]{:S(2)}, u32[]{:S(2)}) collective-permute-start(bf16[520,128]{1,0:T(8,128)(2,1)S(1)} %get-tuple-element.37), channel_id=1, source_target_pairs={{0,28},{4,24},{8,20},{12,16},{16,12},{20,8},{24,4},{28,0},{1,29},{... | collective-permute-start | bytes 399368 | tf_op jit(solution)/shard_map/ppermute | solution.py:21
  42.2 3.5 %collective-permute-start.18 = (bf16[520,128]{1,0:T(8,128)(2,1)S(1)}, bf16[520,128]{1,0:T(8,128)(2,1)S(1)}, u32[]{:S(2)}, u32[]{:S(2)}) collective-permute-start(bf16[520,128]{1,0:T(8,128)(2,1)S(1)} %get-tuple-element.40), channel_id=1, source_target_pairs={{0,4},{4,0},{8,12},{12,8},{16,20},{20,16},{24,28},{28,24},{1,5},{5... | collective-permute-start | bytes 399368 | tf_op jit(solution)/shard_map/ppermute | solution.py:21
  45.7 1.3 %shard_map.74 = (bf16[1,2,256,256]{3,2,1,0:T(8,128)(2,1)S(1)}, f32[8,2,2,128,256]{4,3,2,1,0:T(8,128)S(1)}) custom-call(bf16[32,256]{1,0:T(8,128)(2,1)S(1)} %copy-done.4), custom_call_target="tpu_custom_call" | custom-call | flops 2000000000 | bytes 1048576 | tf_op jit(solution)/shard_map/pallas_call | solution.py:478
  47.0 1.5 %collective-permute-start.13 = (bf16[520,128]{1,0:T(8,128)(2,1)S(1)}, bf16[520,128]{1,0:T(8,128)(2,1)S(1)}, u32[]{:S(2)}, u32[]{:S(2)}) collective-permute-start(bf16[520,128]{1,0:T(8,128)(2,1)S(1)} %get-tuple-element.34), channel_id=1, source_target_pairs={{0,20},{4,16},{8,28},{12,24},{16,4},{20,0},{24,12},{28,8},{1,21},{... | collective-permute-start | bytes 399368 | tf_op jit(solution)/shard_map/ppermute | solution.py:21
  48.5 1.1 %collective-permute-done.16.refs_2_ = bf16[520,128]{1,0:T(8,128)(2,1)S(1)} collective-permute-done((bf16[520,128]{1,0:T(8,128)(2,1)S(1)}, bf16[520,128]{1,0:T(8,128)(2,1)S(1)}, u32[]{:S(2)}, u32[]{:S(2)}) %collective-permute-start.16) | collective-permute-done | bytes 133152 | tf_op jit(solution)/shard_map/ppermute | solution.py:21
  50.3 1.7 %collective-permute-done.17.refs_3_ = bf16[520,128]{1,0:T(8,128)(2,1)S(1)} collective-permute-done((bf16[520,128]{1,0:T(8,128)(2,1)S(1)}, bf16[520,128]{1,0:T(8,128)(2,1)S(1)}, u32[]{:S(2)}, u32[]{:S(2)}) %collective-permute-start.17) | collective-permute-done | bytes 133152 | tf_op jit(solution)/shard_map/ppermute | solution.py:21
  52.0 1.9 %collective-permute-done.18.refs_4_ = bf16[520,128]{1,0:T(8,128)(2,1)S(1)} collective-permute-done((bf16[520,128]{1,0:T(8,128)(2,1)S(1)}, bf16[520,128]{1,0:T(8,128)(2,1)S(1)}, u32[]{:S(2)}, u32[]{:S(2)}) %collective-permute-start.18) | collective-permute-done | bytes 133152 | tf_op jit(solution)/shard_map/ppermute | solution.py:21
  53.8 1.4 %final.4.refs_3_ = bf16[2,1024,256]{2,1,0:T(8,128)(2,1)} custom-call(bf16[520,128]{1,0:T(8,128)(2,1)S(1)} %get-tuple-element.36.refs_0_, bf16[520,128]{1,0:T(8,128)(2,1)S(1)} %collective-permute-done.15.refs_1_, bf16[520,128]{1,0:T(8,128)(2,1)S(1)} %collective-permute-done.16.refs_2_, bf16[520,128]{1,0:T(8,128)(2,1)S(1)} %collective-permute-done.17.refs_3_, ...), custom_call_target="tpu_custom_call" | custom-call | flops 1000000000 | bytes 1048576 | tf_op jit(solution)/shard_map/final/pallas_call | solution.py:541
  55.3 0.9 %final.5.refs_3_ = bf16[2,1024,256]{2,1,0:T(8,128)(2,1)} custom-call(bf16[520,128]{1,0:T(8,128)(2,1)S(1)} %collective-permute-done.14.refs_0_, bf16[1,2,256,256]{3,2,1,0:T(8,128)(2,1)S(1)} %get-tuple-element.32.refs_5_.refs_1_, f32[8,2,2,128,256]{4,3,2,1,0:T(8,128)S(1)} %get-tuple-element.33.refs_6_.refs_2_, ...), custom_call_target="tpu_custom_call", output_to_operand_aliasing={{}: (3, {})} | custom-call | flops 1000000000 | bytes 1048576 | tf_op jit(solution)/shard_map/final/pallas_call | solution.py:541
  56.2 7.7 %collective-permute-done.13.refs_0_ = bf16[520,128]{1,0:T(8,128)(2,1)S(1)} collective-permute-done((bf16[520,128]{1,0:T(8,128)(2,1)S(1)}, bf16[520,128]{1,0:T(8,128)(2,1)S(1)}, u32[]{:S(2)}, u32[]{:S(2)}) %collective-permute-start.13) | collective-permute-done | bytes 133152 | tf_op jit(solution)/shard_map/ppermute | solution.py:21
  (38 shorter events, 4.6 us)
Async XLA Ops:
  2.4 27.2 %copy-start = (bf16[2,256,256]{2,1,0:T(8,128)(2,1)S(1)}, bf16[2,256,256]{2,1,0:T(8,128)(2,1)}, u32[]{:S(2)}) copy-start(bf16[2,256,256]{2,1,0:T(8,128)(2,1)} %refs_2_.1) | copy-start | bytes 786436
  2.4 27.2 %copy-start.1 = (bf16[2,128,512]{2,1,0:T(8,128)(2,1)S(1)}, bf16[2,128,512]{2,1,0:T(8,128)(2,1)}, u32[]{:S(2)}) copy-start(bf16[2,128,512]{2,1,0:T(8,128)(2,1)} %get-tuple-element.23.refs_0_) | copy-start | bytes 786436
  2.4 27.2 %copy-start.2 = (s32[8]{0:T(128)S(1)}, s32[8]{0:T(128)}, u32[]{:S(2)}) copy-start(s32[8]{0:T(128)} %sub_map.3) | copy-start | bytes 100
  2.4 10.1 %collective-permute-start.6 = (bf16[56,256]{1,0:T(8,128)(2,1)}, bf16[56,256]{1,0:T(8,128)(2,1)S(1)}, u32[]{:S(2)}, u32[]{:S(2)}) collective-permute-start(bf16[56,256]{1,0:T(8,128)(2,1)} %get-tuple-element.27.refs_0_), channel_id=1, source_target_pairs={{0,12},{1,9},{2,14},{3,11},{4,8},{5,13},{6,10},{7,15},{8,4},{9,1},... | collective-permute-start | bytes 86024 | tf_op jit(solution)/shard_map/ppermute | solution.py:446
  6.5 7.7 %collective-permute-start.7 = (bf16[56,256]{1,0:T(8,128)(2,1)}, bf16[56,256]{1,0:T(8,128)(2,1)S(1)}, u32[]{:S(2)}, u32[]{:S(2)}) collective-permute-start(bf16[56,256]{1,0:T(8,128)(2,1)} %get-tuple-element.27.refs_0_), channel_id=1, source_target_pairs={{0,4},{2,6},{4,0},{6,2},{8,12},{10,14},{12,8},{14,10},{16,20},{18,... | collective-permute-start | bytes 86024 | tf_op jit(solution)/shard_map/ppermute | solution.py:446
  8.9 6.8 %collective-permute-start.4 = (bf16[56,256]{1,0:T(8,128)(2,1)}, bf16[56,256]{1,0:T(8,128)(2,1)S(1)}, u32[]{:S(2)}, u32[]{:S(2)}) collective-permute-start(bf16[56,256]{1,0:T(8,128)(2,1)} %get-tuple-element.27.refs_0_), channel_id=1, source_target_pairs={{0,28},{1,25},{2,30},{3,27},{4,24},{5,29},{6,26},{7,31},{8,20},{9,... | collective-permute-start | bytes 86024 | tf_op jit(solution)/shard_map/ppermute | solution.py:446
  12.4 6.2 %collective-permute-start.5 = (bf16[56,256]{1,0:T(8,128)(2,1)}, bf16[56,256]{1,0:T(8,128)(2,1)S(1)}, u32[]{:S(2)}, u32[]{:S(2)}) collective-permute-start(bf16[56,256]{1,0:T(8,128)(2,1)} %get-tuple-element.27.refs_0_), channel_id=1, source_target_pairs={{0,20},{1,17},{2,22},{3,19},{4,16},{5,21},{6,18},{7,23},{8,28},{9,... | collective-permute-start | bytes 86024 | tf_op jit(solution)/shard_map/ppermute | solution.py:446
  12.6 12.0 %collective-permute-start.2 = (bf16[2,128,512]{2,1,0:T(8,128)(2,1)}, bf16[2,128,512]{2,1,0:T(8,128)(2,1)S(1)}, u32[]{:S(2)}, u32[]{:S(2)}) collective-permute-start(bf16[2,128,512]{2,1,0:T(8,128)(2,1)} %get-tuple-element.26), channel_id=1, source_target_pairs={{0,3},{1,2},{2,1},{3,0},{4,7},{5,6},{6,5},{7,4},{8,11},{9,10},{10,... | collective-permute-start | bytes 786440 | tf_op jit(solution)/shard_map/ppermute | solution.py:21
  12.6 6.7 %collective-permute-start.10 = (bf16[56,256]{1,0:T(8,128)(2,1)S(1)}, bf16[56,256]{1,0:T(8,128)(2,1)S(1)}, u32[]{:S(2)}, u32[]{:S(2)}) collective-permute-start(bf16[56,256]{1,0:T(8,128)(2,1)S(1)} %collective-permute-done.6.refs_3_), channel_id=1, source_target_pairs={{0,1},{1,0},{2,3},{3,2},{4,5},{5,4},{6,7},{7,6},{8,9},{9,8},{10,11... | collective-permute-start | bytes 86024 | tf_op jit(solution)/shard_map/ppermute | solution.py:21
  14.2 6.6 %collective-permute-start.11 = (bf16[56,256]{1,0:T(8,128)(2,1)S(1)}, bf16[56,256]{1,0:T(8,128)(2,1)S(1)}, u32[]{:S(2)}, u32[]{:S(2)}) collective-permute-start(bf16[56,256]{1,0:T(8,128)(2,1)S(1)} %collective-permute-done.7.refs_4_), channel_id=1, source_target_pairs={{0,1},{1,0},{2,3},{3,2},{4,5},{5,4},{6,7},{7,6},{8,9},{9,8},{10,11... | collective-permute-start | bytes 86024 | tf_op jit(solution)/shard_map/ppermute | solution.py:21
  15.8 5.3 %collective-permute-start.8 = (bf16[56,256]{1,0:T(8,128)(2,1)S(1)}, bf16[56,256]{1,0:T(8,128)(2,1)S(1)}, u32[]{:S(2)}, u32[]{:S(2)}) collective-permute-start(bf16[56,256]{1,0:T(8,128)(2,1)S(1)} %collective-permute-done.4.refs_1_), channel_id=1, source_target_pairs={{0,1},{1,0},{2,3},{3,2},{4,5},{5,4},{6,7},{7,6},{8,9},{9,8},{10,11... | collective-permute-start | bytes 86024 | tf_op jit(solution)/shard_map/ppermute | solution.py:21
  18.6 2.5 %collective-permute-start.9 = (bf16[56,256]{1,0:T(8,128)(2,1)S(1)}, bf16[56,256]{1,0:T(8,128)(2,1)S(1)}, u32[]{:S(2)}, u32[]{:S(2)}) collective-permute-start(bf16[56,256]{1,0:T(8,128)(2,1)S(1)} %collective-permute-done.5.refs_2_), channel_id=1, source_target_pairs={{0,1},{1,0},{2,3},{3,2},{4,5},{5,4},{6,7},{7,6},{8,9},{9,8},{10,11... | collective-permute-start | bytes 86024 | tf_op jit(solution)/shard_map/ppermute | solution.py:21
  19.3 8.9 %collective-permute-start.1 = (bf16[2,128,512]{2,1,0:T(8,128)(2,1)}, bf16[2,128,512]{2,1,0:T(8,128)(2,1)S(1)}, u32[]{:S(2)}, u32[]{:S(2)}) collective-permute-start(bf16[2,128,512]{2,1,0:T(8,128)(2,1)} %get-tuple-element.25), channel_id=1, source_target_pairs={{0,2},{1,3},{2,0},{3,1},{4,6},{5,7},{6,4},{7,5},{8,10},{9,11},{10,... | collective-permute-start | bytes 786440 | tf_op jit(solution)/shard_map/ppermute | solution.py:21
  20.8 7.4 %collective-permute-start = (bf16[2,128,512]{2,1,0:T(8,128)(2,1)}, bf16[2,128,512]{2,1,0:T(8,128)(2,1)S(1)}, u32[]{:S(2)}, u32[]{:S(2)}) collective-permute-start(bf16[2,128,512]{2,1,0:T(8,128)(2,1)} %get-tuple-element.24), channel_id=1, source_target_pairs={{0,1},{1,0},{2,3},{3,2},{4,5},{5,4},{6,7},{7,6},{8,9},{9,8},{10,11... | collective-permute-start | bytes 786440 | tf_op jit(solution)/shard_map/ppermute | solution.py:21
  21.1 0.8 %copy-start.3 = (bf16[56,256]{1,0:T(8,128)(2,1)S(1)}, bf16[56,256]{1,0:T(8,128)(2,1)}, u32[]{:S(2)}) copy-start(bf16[56,256]{1,0:T(8,128)(2,1)} %get-tuple-element.27.refs_0_) | copy-start | bytes 86020
  28.3 6.2 %collective-permute-start.3 = (bf16[4,2,8,512]{3,2,1,0:T(8,128)(2,1)S(1)}, bf16[4,2,8,512]{3,2,1,0:T(8,128)(2,1)S(1)}, u32[]{:S(2)}, u32[]{:S(2)}) collective-permute-start(bf16[4,2,8,512]{3,2,1,0:T(8,128)(2,1)S(1)} %pad_maximum_fusion), channel_id=1, source_target_pairs={{1,28},{2,29},{3,30},{4,0},{5,1},{6,2},{7,3},{8,4},{9,5},{10,6},{1... | collective-permute-start | bytes 196616 | tf_op jit(solution)/shard_map/ppermute | solution.py:475
  34.4 11.3 %copy-start.4 = (bf16[32,256]{1,0:T(8,128)(2,1)S(1)}, bf16[32,256]{1,0:T(8,128)(2,1)}, u32[]{:S(2)}) copy-start(bf16[32,256]{1,0:T(8,128)(2,1)} %get-tuple-element.31.refs_0_) | copy-start | bytes 49156
  37.5 9.5 %collective-permute-start.15 = (bf16[520,128]{1,0:T(8,128)(2,1)S(1)}, bf16[520,128]{1,0:T(8,128)(2,1)S(1)}, u32[]{:S(2)}, u32[]{:S(2)}) collective-permute-start(bf16[520,128]{1,0:T(8,128)(2,1)S(1)} %get-tuple-element.37), channel_id=1, source_target_pairs={{0,28},{4,24},{8,20},{12,16},{16,12},{20,8},{24,4},{28,0},{1,29},{... | collective-permute-start | bytes 399368 | tf_op jit(solution)/shard_map/ppermute | solution.py:21
  42.2 7.5 %collective-permute-start.16 = (bf16[520,128]{1,0:T(8,128)(2,1)S(1)}, bf16[520,128]{1,0:T(8,128)(2,1)S(1)}, u32[]{:S(2)}, u32[]{:S(2)}) collective-permute-start(bf16[520,128]{1,0:T(8,128)(2,1)S(1)} %get-tuple-element.38), channel_id=1, source_target_pairs={{0,12},{4,8},{8,4},{12,0},{16,28},{20,24},{24,20},{28,16},{1,13},{... | collective-permute-start | bytes 399368 | tf_op jit(solution)/shard_map/ppermute | solution.py:21
  42.2 9.8 %collective-permute-start.17 = (bf16[520,128]{1,0:T(8,128)(2,1)S(1)}, bf16[520,128]{1,0:T(8,128)(2,1)S(1)}, u32[]{:S(2)}, u32[]{:S(2)}) collective-permute-start(bf16[520,128]{1,0:T(8,128)(2,1)S(1)} %get-tuple-element.39), channel_id=1, source_target_pairs={{0,8},{4,12},{8,0},{12,4},{16,24},{20,28},{24,16},{28,20},{1,9},{5... | collective-permute-start | bytes 399368 | tf_op jit(solution)/shard_map/ppermute | solution.py:21
  42.2 11.6 %collective-permute-start.18 = (bf16[520,128]{1,0:T(8,128)(2,1)S(1)}, bf16[520,128]{1,0:T(8,128)(2,1)S(1)}, u32[]{:S(2)}, u32[]{:S(2)}) collective-permute-start(bf16[520,128]{1,0:T(8,128)(2,1)S(1)} %get-tuple-element.40), channel_id=1, source_target_pairs={{0,4},{4,0},{8,12},{12,8},{16,20},{20,16},{24,28},{28,24},{1,5},{5... | collective-permute-start | bytes 399368 | tf_op jit(solution)/shard_map/ppermute | solution.py:21
  45.7 9.6 %collective-permute-start.14 = (bf16[520,128]{1,0:T(8,128)(2,1)S(1)}, bf16[520,128]{1,0:T(8,128)(2,1)S(1)}, u32[]{:S(2)}, u32[]{:S(2)}) collective-permute-start(bf16[520,128]{1,0:T(8,128)(2,1)S(1)} %get-tuple-element.35), channel_id=1, source_target_pairs={{0,24},{4,28},{8,16},{12,20},{16,8},{20,12},{24,0},{28,4},{1,25},{... | collective-permute-start | bytes 399368 | tf_op jit(solution)/shard_map/ppermute | solution.py:21
  47.0 16.8 %collective-permute-start.13 = (bf16[520,128]{1,0:T(8,128)(2,1)S(1)}, bf16[520,128]{1,0:T(8,128)(2,1)S(1)}, u32[]{:S(2)}, u32[]{:S(2)}) collective-permute-start(bf16[520,128]{1,0:T(8,128)(2,1)S(1)} %get-tuple-element.34), channel_id=1, source_target_pairs={{0,20},{4,16},{8,28},{12,24},{16,4},{20,0},{24,12},{28,8},{1,21},{... | collective-permute-start | bytes 399368 | tf_op jit(solution)/shard_map/ppermute | solution.py:21
  49.7 15.3 %collective-permute-start.12 = (bf16[520,128]{1,0:T(8,128)(2,1)S(1)}, bf16[520,128]{1,0:T(8,128)(2,1)S(1)}, u32[]{:S(2)}, u32[]{:S(2)}) collective-permute-start(bf16[520,128]{1,0:T(8,128)(2,1)S(1)} %get-tuple-element.30), channel_id=1, source_target_pairs={{0,16},{4,20},{8,24},{12,28},{16,0},{20,4},{24,8},{28,12},{1,17},{... | collective-permute-start | bytes 399368 | tf_op jit(solution)/shard_map/ppermute | solution.py:21
where the time goes:
time: 66.2 us; the launch traced here: 65.9 us
  starting transfers between devices  25.2 us (38%)
  waiting for transfers between devices  23.3 us (35%)
  Pallas kernels  15.6 us (24%)
  local copies, waits for them, and re-layouts  1.5 us (2%)
    ppermute x14, waiting for transfers between devices, exchanged(): lax.ppermute(block, axis, [(source, source ^ mask) for source in range(co...  16.2 us
    ppermute x14, starting transfers between devices, exchanged(): lax.ppermute(block, axis, [(source, source ^ mask) for source in range(co...  13.8 us
    ppermute x4, starting transfers between devices, on_device(): mine.append(lax.ppermute(early_pack, ('sub', 'rng'), route))  10.1 us
    ppermute x4, waiting for transfers between devices, on_device(): mine.append(lax.ppermute(early_pack, ('sub', 'rng'), route))  4.28 us
    pallas_call x4, Pallas kernels, on_device(): pl.pallas_call(functools.partial(final_kernel, chosen, group, rows, resul...  4.14 us
    pallas_call x2, Pallas kernels, tables(): pl.pallas_call(functools.partial(table_kernel, group, terms, sources, tap...  4.02 us
    pallas_call x1, Pallas kernels, on_device(): pl.pallas_call(functools.partial(merge_kernel, group, segments, rows, pul...  3.07 us
    ppermute x1, waiting for transfers between devices, on_device(): edge = lax.ppermute(edge_rows, ('sub', 'rng'), route)  2.79 us
  transfers between devices with their start and end apart: 19, of which 9 were waited for; matrix products, arithmetic and copies ran while one was open for 1% of the time, Pallas kernels for 14%

commit v1 on v0

--- a/solution.py
+++ b/solution.py
@@ -236,14 +236,18 @@
     half = image.shape[-1]
     per_source = group // sources
     slab = lax.axis_index("rng")
-    for source in range(sources):
-        for piece in range(per_source):
-            columns = slice(piece * pulse_count, (piece + 1) * pulse_count)
+
+    def step(piece, carry):
+        columns = pl.ds(pl.multiple_of(piece * pulse_count, pulse_count), pulse_count)
+        for source in range(sources):
             target = place_of(sub_map, group, sources, slab, source * per_source + piece)
             parts = [blocks[source][c, :, columns] for c in range(2)]
             for c, value in enumerate(formed(steering, *parts)):
                 for window in range(2):
                     image[target, c, window] = value[:, window * half : (window + 1) * half]
+        return carry
+
+    lax.fori_loop(0, per_source, step, 0)
 
 
 def turned(values, block):
@@ -416,19 +420,16 @@
     tables_in = (band_offset, interp_weight, range_frac, phase_rate)
     *quarters, early_pack, late_pack = pl.pallas_call(
         functools.partial(cut_kernel, slabs, segments, taps, half),
-        out_shape=[jax.ShapeDtypeStruct(cut, jnp.bfloat16)] * slabs
-        + [
-            jax.ShapeDtypeStruct((pack_rows(terms, taps), angles), jnp.bfloat16)
-            for terms in (early, late)
-        ],
+        out_shape=[pltpu.VMEM(cut, jnp.bfloat16)] * slabs
+        + [pltpu.VMEM((pack_rows(terms, taps), angles), jnp.bfloat16) for terms in (early, late)],
         in_specs=[FAR] * 5,
         out_specs=[WHOLE] * (slabs + 2),
         scratch_shapes=[pltpu.VMEM(value.shape, value.dtype) for value in tables_in]
         + [pltpu.SemaphoreType.DMA((slabs, 2)), pltpu.SemaphoreType.DMA((4,))],
-        compiler_params=params(60),
+        compiler_params=params(2),
         cost_estimate=cost(1_000_000_000),
         name="cut",
-    )(echoes, *tables_in)
+    )(*[pltpu.with_memory_space_constraint(value, pltpu.HBM) for value in (echoes,) + tables_in])
 
     received = [quarters[0]] + [None] * (slabs - 1)
     for mask in range(slabs - 1, 0, -1):

time: 66.2 us -> 64.9 us (0.980)
  the two profiles are of different devices: /device:TPU:0 before, /device:TPU:1 now
where the time goes in v1:
time: 64.9 us; the launch traced here: 63.6 us
  starting transfers between devices  32.6 us (50%)
  waiting for transfers between devices  16 us (25%)
  Pallas kernels  14.8 us (23%)
    ppermute x14, starting transfers between devices, exchanged(): lax.ppermute(block, axis, [(source, source ^ mask) for source in range(co...  21.4 us
    ppermute x14, waiting for transfers between devices, exchanged(): lax.ppermute(block, axis, [(source, source ^ mask) for source in range(co...  16 us
    ppermute x1, starting transfers between devices, on_device(): edge = lax.ppermute(edge_rows, ('sub', 'rng'), route)  5.9 us
    ppermute x4, starting transfers between devices, on_device(): mine.append(lax.ppermute(early_pack, ('sub', 'rng'), route))  5.28 us
    pallas_call x4, Pallas kernels, on_device(): pl.pallas_call(functools.partial(final_kernel, chosen, group, rows, resul...  4.14 us
    pallas_call x2, Pallas kernels, tables(): pl.pallas_call(functools.partial(table_kernel, group, terms, sources, tap...  4.03 us
    pallas_call x1, Pallas kernels, on_device(): pl.pallas_call(functools.partial(merge_kernel, group, segments, rows, pul...  3.07 us
    pallas_call x1, Pallas kernels, on_device(): pl.pallas_call(functools.partial(form_kernel, group, pulse_count, len(blo...  2.17 us
  transfers between devices with their start and end apart: 19, of which 6 were waited for; matrix products, arithmetic and copies ran while one was open for 0% of the time, Pallas kernels for 15%

profile of v1, /device:TPU:1, one launch (start us, length us, event | category | flops | bytes accessed | tf_op | source)
XLA Modules:
  0.0 63.6 jit_solution(12229997492160381595)
XLA Ops:
  0.0 1.4 %cut.1 = (bf16[2,128,512]{2,1,0:T(8,128)(2,1)S(1)}, bf16[2,128,512]{2,1,0:T(8,128)(2,1)S(1)}, bf16[2,128,512]{2,1,0:T(8,128)(2,1)S(1)}, bf16[2,128,512]{2,1,0:T(...) custom-call(bf16[2,4,128,512]{3,2,1,0:T(8,128)(2,1)} %echoes.1, s32[1,3,2,256]{3,2,1,0:T(2,128)} %offset.1, ...), custom_call_target="tpu_custom_call" | custom-call | flops 1000000000 | bytes 1048576 | tf_op jit(solution)/shard_map/cut/pallas_call | solution.py:421
  1.5 2.2 %collective-permute-start.6 = (bf16[56,256]{1,0:T(8,128)(2,1)S(1)}, bf16[56,256]{1,0:T(8,128)(2,1)S(1)}, u32[]{:S(2)}, u32[]{:S(2)}) collective-permute-start(bf16[56,256]{1,0:T(8,128)(2,1)S(1)} %get-tuple-element.27.refs_0_), channel_id=1, source_target_pairs={{0,12},{1,9},{2,14},{3,11},{4,8},{5,13},{6,10},{7,15},{8,4},{9,1},... | collective-permute-start | bytes 86024 | tf_op jit(solution)/shard_map/ppermute | solution.py:447
  4.3 2.3 %collective-permute-start.4 = (bf16[56,256]{1,0:T(8,128)(2,1)S(1)}, bf16[56,256]{1,0:T(8,128)(2,1)S(1)}, u32[]{:S(2)}, u32[]{:S(2)}) collective-permute-start(bf16[56,256]{1,0:T(8,128)(2,1)S(1)} %get-tuple-element.27.refs_0_), channel_id=1, source_target_pairs={{0,28},{1,25},{2,30},{3,27},{4,24},{5,29},{6,26},{7,31},{8,20},{9,... | collective-permute-start | bytes 86024 | tf_op jit(solution)/shard_map/ppermute | solution.py:447
  6.7 6.0 %collective-permute-start.2 = (bf16[2,128,512]{2,1,0:T(8,128)(2,1)S(1)}, bf16[2,128,512]{2,1,0:T(8,128)(2,1)S(1)}, u32[]{:S(2)}, u32[]{:S(2)}) collective-permute-start(bf16[2,128,512]{2,1,0:T(8,128)(2,1)S(1)} %get-tuple-element.26), channel_id=1, source_target_pairs={{0,3},{1,2},{2,1},{3,0},{4,7},{5,6},{6,5},{7,4},{8,11},{9,10},{10,... | collective-permute-start | bytes 786440 | tf_op jit(solution)/shard_map/ppermute | solution.py:21
  13.3 1.3 %collective-permute-start.8 = (bf16[56,256]{1,0:T(8,128)(2,1)S(1)}, bf16[56,256]{1,0:T(8,128)(2,1)S(1)}, u32[]{:S(2)}, u32[]{:S(2)}) collective-permute-start(bf16[56,256]{1,0:T(8,128)(2,1)S(1)} %collective-permute-done.4.refs_1_), channel_id=1, source_target_pairs={{0,1},{1,0},{2,3},{3,2},{4,5},{5,4},{6,7},{7,6},{8,9},{9,8},{10,11... | collective-permute-start | bytes 86024 | tf_op jit(solution)/shard_map/ppermute | solution.py:21
  14.6 2.8 %collective-permute-start.9 = (bf16[56,256]{1,0:T(8,128)(2,1)S(1)}, bf16[56,256]{1,0:T(8,128)(2,1)S(1)}, u32[]{:S(2)}, u32[]{:S(2)}) collective-permute-start(bf16[56,256]{1,0:T(8,128)(2,1)S(1)} %collective-permute-done.5.refs_2_), channel_id=1, source_target_pairs={{0,1},{1,0},{2,3},{3,2},{4,5},{5,4},{6,7},{7,6},{8,9},{9,8},{10,11... | collective-permute-start | bytes 86024 | tf_op jit(solution)/shard_map/ppermute | solution.py:21
  17.4 1.2 %collective-permute-start.1 = (bf16[2,128,512]{2,1,0:T(8,128)(2,1)S(1)}, bf16[2,128,512]{2,1,0:T(8,128)(2,1)S(1)}, u32[]{:S(2)}, u32[]{:S(2)}) collective-permute-start(bf16[2,128,512]{2,1,0:T(8,128)(2,1)S(1)} %get-tuple-element.25), channel_id=1, source_target_pairs={{0,2},{1,3},{2,0},{3,1},{4,6},{5,7},{6,4},{7,5},{8,10},{9,11},{10,... | collective-permute-start | bytes 786440 | tf_op jit(solution)/shard_map/ppermute | solution.py:21
  19.0 2.7 %shard_map.73 = (bf16[8,4,256,256]{3,2,1,0:T(8,128)(2,1)S(1)}, f32[8,4,2,136,256]{4,3,2,1,0:T(8,128)S(1)}) custom-call(bf16[56,256]{1,0:T(8,128)(2,1)S(1)} %get-tuple-element.27.refs_0_, bf16[56,256]{1,0:T(8,128)(2,1)S(1)} %collective-permute-done.4.refs_1_, bf16[56,256]{1,0:T(8,128)(2,1)S(1)} %collective-permute-done.5.refs_2_, ...), custom_call_target="tpu_custom_call" | custom-call | flops 2000000000 | bytes 1048576 | tf_op jit(solution)/shard_map/pallas_call | solution.py:479
  21.8 3.4 %collective-permute-done.1.refs_2_ = bf16[2,128,512]{2,1,0:T(8,128)(2,1)S(1)} collective-permute-done((bf16[2,128,512]{2,1,0:T(8,128)(2,1)S(1)}, bf16[2,128,512]{2,1,0:T(8,128)(2,1)S(1)}, u32[]{:S(2)}, u32[]{:S(2)}) %collective-permute-start.1) | collective-permute-done | bytes 262176 | tf_op jit(solution)/shard_map/ppermute | solution.py:21
  25.2 5.9 %collective-permute-start.3 = (bf16[4,2,8,512]{3,2,1,0:T(8,128)(2,1)S(1)}, bf16[4,2,8,512]{3,2,1,0:T(8,128)(2,1)S(1)}, u32[]{:S(2)}, u32[]{:S(2)}) collective-permute-start(bf16[4,2,8,512]{3,2,1,0:T(8,128)(2,1)S(1)} %pad_maximum_fusion), channel_id=1, source_target_pairs={{1,28},{2,29},{3,30},{4,0},{5,1},{6,2},{7,3},{8,4},{9,5},{10,6},{1... | collective-permute-start | bytes 196616 | tf_op jit(solution)/shard_map/ppermute | solution.py:476
  31.2 2.2 %form.1.refs_0_ = f32[8,2,2,128,128]{4,3,2,1,0:T(8,128)S(1)} custom-call(s32[8]{0:T(128)S(1)} %copy-done.1, bf16[2,128,512]{2,1,0:T(8,128)(2,1)S(1)} %get-tuple-element.23.refs_0_, bf16[2,128,512]{2,1,0:T(8,128)(2,1)S(1)} %collective-permute-done.refs_1_, bf16[2,128,512]{2,1,0:T(8,128)(2,1)S(1)} %collective-permute-done.1.refs_2_, ...), custom_call_target="tpu_custom_call" | custom-call | flops 1000000000 | bytes 1048576 | tf_op jit(solution)/shard_map/form/pallas_call | solution.py:509
  33.3 3.1 %merge.1 = (bf16[520,128]{1,0:T(8,128)(2,1)S(1)}, bf16[520,128]{1,0:T(8,128)(2,1)S(1)}, bf16[520,128]{1,0:T(8,128)(2,1)S(1)}, bf16[520,128]{1,0:T(8,128)(2,1)S(1...) custom-call(s32[8]{0:T(128)S(1)} %copy-done.1, ...), custom_call_target="tpu_custom_call" | custom-call | flops 4000000000 | bytes 1048576 | tf_op jit(solution)/shard_map/merge/pallas_call | solution.py:519
  36.4 4.8 %collective-permute-start.15 = (bf16[520,128]{1,0:T(8,128)(2,1)S(1)}, bf16[520,128]{1,0:T(8,128)(2,1)S(1)}, u32[]{:S(2)}, u32[]{:S(2)}) collective-permute-start(bf16[520,128]{1,0:T(8,128)(2,1)S(1)} %get-tuple-element.37), channel_id=1, source_target_pairs={{0,28},{4,24},{8,20},{12,16},{16,12},{20,8},{24,4},{28,0},{1,29},{... | collective-permute-start | bytes 399368 | tf_op jit(solution)/shard_map/ppermute | solution.py:21
  41.2 2.6 %collective-permute-start.18 = (bf16[520,128]{1,0:T(8,128)(2,1)S(1)}, bf16[520,128]{1,0:T(8,128)(2,1)S(1)}, u32[]{:S(2)}, u32[]{:S(2)}) collective-permute-start(bf16[520,128]{1,0:T(8,128)(2,1)S(1)} %get-tuple-element.40), channel_id=1, source_target_pairs={{0,4},{4,0},{8,12},{12,8},{16,20},{20,16},{24,28},{28,24},{1,5},{5... | collective-permute-start | bytes 399368 | tf_op jit(solution)/shard_map/ppermute | solution.py:21
  43.8 1.3 %shard_map.74 = (bf16[1,2,256,256]{3,2,1,0:T(8,128)(2,1)S(1)}, f32[8,2,2,128,256]{4,3,2,1,0:T(8,128)S(1)}) custom-call(bf16[32,256]{1,0:T(8,128)(2,1)S(1)} %get-tuple-element.31.refs_0_), custom_call_target="tpu_custom_call" | custom-call | flops 2000000000 | bytes 1048576 | tf_op jit(solution)/shard_map/pallas_call | solution.py:479
  45.1 1.2 %collective-permute-start.13 = (bf16[520,128]{1,0:T(8,128)(2,1)S(1)}, bf16[520,128]{1,0:T(8,128)(2,1)S(1)}, u32[]{:S(2)}, u32[]{:S(2)}) collective-permute-start(bf16[520,128]{1,0:T(8,128)(2,1)S(1)} %get-tuple-element.34), channel_id=1, source_target_pairs={{0,20},{4,16},{8,28},{12,24},{16,4},{20,0},{24,12},{28,8},{1,21},{... | collective-permute-start | bytes 399368 | tf_op jit(solution)/shard_map/ppermute | solution.py:21
  46.4 1.5 %collective-permute-done.16.refs_2_ = bf16[520,128]{1,0:T(8,128)(2,1)S(1)} collective-permute-done((bf16[520,128]{1,0:T(8,128)(2,1)S(1)}, bf16[520,128]{1,0:T(8,128)(2,1)S(1)}, u32[]{:S(2)}, u32[]{:S(2)}) %collective-permute-start.16) | collective-permute-done | bytes 133152 | tf_op jit(solution)/shard_map/ppermute | solution.py:21
  48.5 1.9 %collective-permute-done.17.refs_3_ = bf16[520,128]{1,0:T(8,128)(2,1)S(1)} collective-permute-done((bf16[520,128]{1,0:T(8,128)(2,1)S(1)}, bf16[520,128]{1,0:T(8,128)(2,1)S(1)}, u32[]{:S(2)}, u32[]{:S(2)}) %collective-permute-start.17) | collective-permute-done | bytes 133152 | tf_op jit(solution)/shard_map/ppermute | solution.py:21
  50.4 1.8 %collective-permute-done.18.refs_4_ = bf16[520,128]{1,0:T(8,128)(2,1)S(1)} collective-permute-done((bf16[520,128]{1,0:T(8,128)(2,1)S(1)}, bf16[520,128]{1,0:T(8,128)(2,1)S(1)}, u32[]{:S(2)}, u32[]{:S(2)}) %collective-permute-start.18) | collective-permute-done | bytes 133152 | tf_op jit(solution)/shard_map/ppermute | solution.py:21
  52.2 1.4 %final.4.refs_3_ = bf16[2,1024,256]{2,1,0:T(8,128)(2,1)} custom-call(bf16[520,128]{1,0:T(8,128)(2,1)S(1)} %get-tuple-element.36.refs_0_, bf16[520,128]{1,0:T(8,128)(2,1)S(1)} %collective-permute-done.15.refs_1_, bf16[520,128]{1,0:T(8,128)(2,1)S(1)} %collective-permute-done.16.refs_2_, bf16[520,128]{1,0:T(8,128)(2,1)S(1)} %collective-permute-done.17.refs_3_, ...), custom_call_target="tpu_custom_call" | custom-call | flops 1000000000 | bytes 1048576 | tf_op jit(solution)/shard_map/final/pallas_call | solution.py:542
  53.6 0.9 %final.5.refs_3_ = bf16[2,1024,256]{2,1,0:T(8,128)(2,1)} custom-call(bf16[520,128]{1,0:T(8,128)(2,1)S(1)} %collective-permute-done.14.refs_0_, bf16[1,2,256,256]{3,2,1,0:T(8,128)(2,1)S(1)} %get-tuple-element.32.refs_5_.refs_1_, f32[8,2,2,128,256]{4,3,2,1,0:T(8,128)S(1)} %get-tuple-element.33.refs_6_.refs_2_, ...), custom_call_target="tpu_custom_call", output_to_operand_aliasing={{}: (3, {})} | custom-call | flops 1000000000 | bytes 1048576 | tf_op jit(solution)/shard_map/final/pallas_call | solution.py:542
  54.6 5.5 %collective-permute-done.13.refs_0_ = bf16[520,128]{1,0:T(8,128)(2,1)S(1)} collective-permute-done((bf16[520,128]{1,0:T(8,128)(2,1)S(1)}, bf16[520,128]{1,0:T(8,128)(2,1)S(1)}, u32[]{:S(2)}, u32[]{:S(2)}) %collective-permute-start.13) | collective-permute-done | bytes 133152 | tf_op jit(solution)/shard_map/ppermute | solution.py:21
  60.1 0.9 %final.6.refs_3_ = bf16[2,1024,256]{2,1,0:T(8,128)(2,1)} custom-call(bf16[520,128]{1,0:T(8,128)(2,1)S(1)} %collective-permute-done.13.refs_0_, bf16[1,2,256,256]{3,2,1,0:T(8,128)(2,1)S(1)} %get-tuple-element.32.refs_5_.refs_1_, f32[8,2,2,128,256]{4,3,2,1,0:T(8,128)S(1)} %get-tuple-element.33.refs_6_.refs_2_, ...), custom_call_target="tpu_custom_call", output_to_operand_aliasing={{}: (3, {})} | custom-call | flops 1000000000 | bytes 1048576 | tf_op jit(solution)/shard_map/final/pallas_call | solution.py:542
  61.0 1.7 %collective-permute-done.12.refs_0_ = bf16[520,128]{1,0:T(8,128)(2,1)S(1)} collective-permute-done((bf16[520,128]{1,0:T(8,128)(2,1)S(1)}, bf16[520,128]{1,0:T(8,128)(2,1)S(1)}, u32[]{:S(2)}, u32[]{:S(2)}) %collective-permute-start.12) | collective-permute-done | bytes 133152 | tf_op jit(solution)/shard_map/ppermute | solution.py:21
  (32 shorter events, 3.2 us)
Async XLA Ops:
  1.4 29.7 %copy-start = (bf16[2,256,256]{2,1,0:T(8,128)(2,1)S(1)}, bf16[2,256,256]{2,1,0:T(8,128)(2,1)}, u32[]{:S(2)}) copy-start(bf16[2,256,256]{2,1,0:T(8,128)(2,1)} %refs_2_.1) | copy-start | bytes 786436
  1.4 29.7 %copy-start.1 = (s32[8]{0:T(128)S(1)}, s32[8]{0:T(128)}, u32[]{:S(2)}) copy-start(s32[8]{0:T(128)} %sub_map.3) | copy-start | bytes 100
  1.5 11.3 %collective-permute-start.6 = (bf16[56,256]{1,0:T(8,128)(2,1)S(1)}, bf16[56,256]{1,0:T(8,128)(2,1)S(1)}, u32[]{:S(2)}, u32[]{:S(2)}) collective-permute-start(bf16[56,256]{1,0:T(8,128)(2,1)S(1)} %get-tuple-element.27.refs_0_), channel_id=1, source_target_pairs={{0,12},{1,9},{2,14},{3,11},{4,8},{5,13},{6,10},{7,15},{8,4},{9,1},... | collective-permute-start | bytes 86024 | tf_op jit(solution)/shard_map/ppermute | solution.py:447
  3.6 9.1 %collective-permute-start.7 = (bf16[56,256]{1,0:T(8,128)(2,1)S(1)}, bf16[56,256]{1,0:T(8,128)(2,1)S(1)}, u32[]{:S(2)}, u32[]{:S(2)}) collective-permute-start(bf16[56,256]{1,0:T(8,128)(2,1)S(1)} %get-tuple-element.27.refs_0_), channel_id=1, source_target_pairs={{0,4},{2,6},{4,0},{6,2},{8,12},{10,14},{12,8},{14,10},{16,20},{18,... | collective-permute-start | bytes 86024 | tf_op jit(solution)/shard_map/ppermute | solution.py:447
  4.3 9.0 %collective-permute-start.4 = (bf16[56,256]{1,0:T(8,128)(2,1)S(1)}, bf16[56,256]{1,0:T(8,128)(2,1)S(1)}, u32[]{:S(2)}, u32[]{:S(2)}) collective-permute-start(bf16[56,256]{1,0:T(8,128)(2,1)S(1)} %get-tuple-element.27.refs_0_), channel_id=1, source_target_pairs={{0,28},{1,25},{2,30},{3,27},{4,24},{5,29},{6,26},{7,31},{8,20},{9,... | collective-permute-start | bytes 86024 | tf_op jit(solution)/shard_map/ppermute | solution.py:447
  6.6 8.0 %collective-permute-start.5 = (bf16[56,256]{1,0:T(8,128)(2,1)S(1)}, bf16[56,256]{1,0:T(8,128)(2,1)S(1)}, u32[]{:S(2)}, u32[]{:S(2)}) collective-permute-start(bf16[56,256]{1,0:T(8,128)(2,1)S(1)} %get-tuple-element.27.refs_0_), channel_id=1, source_target_pairs={{0,20},{1,17},{2,22},{3,19},{4,16},{5,21},{6,18},{7,23},{8,28},{9,... | collective-permute-start | bytes 86024 | tf_op jit(solution)/shard_map/ppermute | solution.py:447
  6.7 15.0 %collective-permute-start.2 = (bf16[2,128,512]{2,1,0:T(8,128)(2,1)S(1)}, bf16[2,128,512]{2,1,0:T(8,128)(2,1)S(1)}, u32[]{:S(2)}, u32[]{:S(2)}) collective-permute-start(bf16[2,128,512]{2,1,0:T(8,128)(2,1)S(1)} %get-tuple-element.26), channel_id=1, source_target_pairs={{0,3},{1,2},{2,1},{3,0},{4,7},{5,6},{6,5},{7,4},{8,11},{9,10},{10,... | collective-permute-start | bytes 786440 | tf_op jit(solution)/shard_map/ppermute | solution.py:21
  12.7 4.7 %collective-permute-start.10 = (bf16[56,256]{1,0:T(8,128)(2,1)S(1)}, bf16[56,256]{1,0:T(8,128)(2,1)S(1)}, u32[]{:S(2)}, u32[]{:S(2)}) collective-permute-start(bf16[56,256]{1,0:T(8,128)(2,1)S(1)} %collective-permute-done.6.refs_3_), channel_id=1, source_target_pairs={{0,1},{1,0},{2,3},{3,2},{4,5},{5,4},{6,7},{7,6},{8,9},{9,8},{10,11... | collective-permute-start | bytes 86024 | tf_op jit(solution)/shard_map/ppermute | solution.py:21
  12.8 5.9 %collective-permute-start.11 = (bf16[56,256]{1,0:T(8,128)(2,1)S(1)}, bf16[56,256]{1,0:T(8,128)(2,1)S(1)}, u32[]{:S(2)}, u32[]{:S(2)}) collective-permute-start(bf16[56,256]{1,0:T(8,128)(2,1)S(1)} %collective-permute-done.7.refs_4_), channel_id=1, source_target_pairs={{0,1},{1,0},{2,3},{3,2},{4,5},{5,4},{6,7},{7,6},{8,9},{9,8},{10,11... | collective-permute-start | bytes 86024 | tf_op jit(solution)/shard_map/ppermute | solution.py:21
  13.3 5.7 %collective-permute-start.8 = (bf16[56,256]{1,0:T(8,128)(2,1)S(1)}, bf16[56,256]{1,0:T(8,128)(2,1)S(1)}, u32[]{:S(2)}, u32[]{:S(2)}) collective-permute-start(bf16[56,256]{1,0:T(8,128)(2,1)S(1)} %collective-permute-done.4.refs_1_), channel_id=1, source_target_pairs={{0,1},{1,0},{2,3},{3,2},{4,5},{5,4},{6,7},{7,6},{8,9},{9,8},{10,11... | collective-permute-start | bytes 86024 | tf_op jit(solution)/shard_map/ppermute | solution.py:21
  14.6 4.4 %collective-permute-start.9 = (bf16[56,256]{1,0:T(8,128)(2,1)S(1)}, bf16[56,256]{1,0:T(8,128)(2,1)S(1)}, u32[]{:S(2)}, u32[]{:S(2)}) collective-permute-start(bf16[56,256]{1,0:T(8,128)(2,1)S(1)} %collective-permute-done.5.refs_2_), channel_id=1, source_target_pairs={{0,1},{1,0},{2,3},{3,2},{4,5},{5,4},{6,7},{7,6},{8,9},{9,8},{10,11... | collective-permute-start | bytes 86024 | tf_op jit(solution)/shard_map/ppermute | solution.py:21
  17.4 7.8 %collective-permute-start.1 = (bf16[2,128,512]{2,1,0:T(8,128)(2,1)S(1)}, bf16[2,128,512]{2,1,0:T(8,128)(2,1)S(1)}, u32[]{:S(2)}, u32[]{:S(2)}) collective-permute-start(bf16[2,128,512]{2,1,0:T(8,128)(2,1)S(1)} %get-tuple-element.25), channel_id=1, source_target_pairs={{0,2},{1,3},{2,0},{3,1},{4,6},{5,7},{6,4},{7,5},{8,10},{9,11},{10,... | collective-permute-start | bytes 786440 | tf_op jit(solution)/shard_map/ppermute | solution.py:21
  18.6 6.6 %collective-permute-start = (bf16[2,128,512]{2,1,0:T(8,128)(2,1)S(1)}, bf16[2,128,512]{2,1,0:T(8,128)(2,1)S(1)}, u32[]{:S(2)}, u32[]{:S(2)}) collective-permute-start(bf16[2,128,512]{2,1,0:T(8,128)(2,1)S(1)} %get-tuple-element.24), channel_id=1, source_target_pairs={{0,1},{1,0},{2,3},{3,2},{4,5},{5,4},{6,7},{7,6},{8,9},{9,8},{10,11... | collective-permute-start | bytes 786440 | tf_op jit(solution)/shard_map/ppermute | solution.py:21
  25.2 8.1 %collective-permute-start.3 = (bf16[4,2,8,512]{3,2,1,0:T(8,128)(2,1)S(1)}, bf16[4,2,8,512]{3,2,1,0:T(8,128)(2,1)S(1)}, u32[]{:S(2)}, u32[]{:S(2)}) collective-permute-start(bf16[4,2,8,512]{3,2,1,0:T(8,128)(2,1)S(1)} %pad_maximum_fusion), channel_id=1, source_target_pairs={{1,28},{2,29},{3,30},{4,0},{5,1},{6,2},{7,3},{8,4},{9,5},{10,6},{1... | collective-permute-start | bytes 196616 | tf_op jit(solution)/shard_map/ppermute | solution.py:476
  36.4 8.7 %collective-permute-start.15 = (bf16[520,128]{1,0:T(8,128)(2,1)S(1)}, bf16[520,128]{1,0:T(8,128)(2,1)S(1)}, u32[]{:S(2)}, u32[]{:S(2)}) collective-permute-start(bf16[520,128]{1,0:T(8,128)(2,1)S(1)} %get-tuple-element.37), channel_id=1, source_target_pairs={{0,28},{4,24},{8,20},{12,16},{16,12},{20,8},{24,4},{28,0},{1,29},{... | collective-permute-start | bytes 399368 | tf_op jit(solution)/shard_map/ppermute | solution.py:21
  41.2 6.8 %collective-permute-start.16 = (bf16[520,128]{1,0:T(8,128)(2,1)S(1)}, bf16[520,128]{1,0:T(8,128)(2,1)S(1)}, u32[]{:S(2)}, u32[]{:S(2)}) collective-permute-start(bf16[520,128]{1,0:T(8,128)(2,1)S(1)} %get-tuple-element.38), channel_id=1, source_target_pairs={{0,12},{4,8},{8,4},{12,0},{16,28},{20,24},{24,20},{28,16},{1,13},{... | collective-permute-start | bytes 399368 | tf_op jit(solution)/shard_map/ppermute | solution.py:21
  41.2 9.2 %collective-permute-start.17 = (bf16[520,128]{1,0:T(8,128)(2,1)S(1)}, bf16[520,128]{1,0:T(8,128)(2,1)S(1)}, u32[]{:S(2)}, u32[]{:S(2)}) collective-permute-start(bf16[520,128]{1,0:T(8,128)(2,1)S(1)} %get-tuple-element.39), channel_id=1, source_target_pairs={{0,8},{4,12},{8,0},{12,4},{16,24},{20,28},{24,16},{28,20},{1,9},{5... | collective-permute-start | bytes 399368 | tf_op jit(solution)/shard_map/ppermute | solution.py:21
  41.2 11.0 %collective-permute-start.18 = (bf16[520,128]{1,0:T(8,128)(2,1)S(1)}, bf16[520,128]{1,0:T(8,128)(2,1)S(1)}, u32[]{:S(2)}, u32[]{:S(2)}) collective-permute-start(bf16[520,128]{1,0:T(8,128)(2,1)S(1)} %get-tuple-element.40), channel_id=1, source_target_pairs={{0,4},{4,0},{8,12},{12,8},{16,20},{20,16},{24,28},{28,24},{1,5},{5... | collective-permute-start | bytes 399368 | tf_op jit(solution)/shard_map/ppermute | solution.py:21
  43.8 9.8 %collective-permute-start.14 = (bf16[520,128]{1,0:T(8,128)(2,1)S(1)}, bf16[520,128]{1,0:T(8,128)(2,1)S(1)}, u32[]{:S(2)}, u32[]{:S(2)}) collective-permute-start(bf16[520,128]{1,0:T(8,128)(2,1)S(1)} %get-tuple-element.35), channel_id=1, source_target_pairs={{0,24},{4,28},{8,16},{12,20},{16,8},{20,12},{24,0},{28,4},{1,25},{... | collective-permute-start | bytes 399368 | tf_op jit(solution)/shard_map/ppermute | solution.py:21
  45.1 14.9 %collective-permute-start.13 = (bf16[520,128]{1,0:T(8,128)(2,1)S(1)}, bf16[520,128]{1,0:T(8,128)(2,1)S(1)}, u32[]{:S(2)}, u32[]{:S(2)}) collective-permute-start(bf16[520,128]{1,0:T(8,128)(2,1)S(1)} %get-tuple-element.34), channel_id=1, source_target_pairs={{0,20},{4,16},{8,28},{12,24},{16,4},{20,0},{24,12},{28,8},{1,21},{... | collective-permute-start | bytes 399368 | tf_op jit(solution)/shard_map/ppermute | solution.py:21
  47.9 14.8 %collective-permute-start.12 = (bf16[520,128]{1,0:T(8,128)(2,1)S(1)}, bf16[520,128]{1,0:T(8,128)(2,1)S(1)}, u32[]{:S(2)}, u32[]{:S(2)}) collective-permute-start(bf16[520,128]{1,0:T(8,128)(2,1)S(1)} %get-tuple-element.30), channel_id=1, source_target_pairs={{0,16},{4,20},{8,24},{12,28},{16,0},{20,4},{24,8},{28,12},{1,17},{... | collective-permute-start | bytes 399368 | tf_op jit(solution)/shard_map/ppermute | solution.py:21

commit v2 on v1

--- a/solution.py
+++ b/solution.py
@@ -64,7 +64,10 @@
         copy.wait()
     offset, weight, fraction, rate = held
     angles = weight.shape[-1]
-    for pack, chosen in ((packs[0], range(segments - 1)), (packs[1], (segments - 1,))):
+    for copies_of, chosen in (
+        ([packs[0].at[index] for index in range(group)], range(segments - 1)),
+        ([packs[1]], (segments - 1,)),
+    ):
         kinds = [[] for _ in range(KINDS)]
         terms = 2 * len(chosen)
         for index, segment in enumerate(chosen):
@@ -80,26 +83,27 @@
                     slot += 1
             for child in range(2):
                 term = index * 2 + child
-                pack[term * taps : (term + 1) * taps, :] = weight[0, segment, child]
+                for pack in copies_of:
+                    pack[term * taps : (term + 1) * taps, :] = weight[0, segment, child]
         rows = [piece for kind in kinds for piece in kind]
         padding = pack_rows(terms, taps) - terms * (taps + KINDS)
         if padding:
             rows.append(jnp.zeros((padding, angles), jnp.float32))
-        pack[terms * taps :, :] = jnp.concatenate(rows, axis=0).astype(jnp.bfloat16)
+        tail = jnp.concatenate(rows, axis=0).astype(jnp.bfloat16)
+        for pack in copies_of:
+            pack[terms * taps :, :] = tail
     for copy in copies:
         copy.wait()
 
 
-def table_kernel(members, terms, masks, taps, half, rows, lines, range_rows, total_range, *refs):
-    steps = len(masks[0]) if masks else 0
-    own, mine, theirs = refs[0], refs[1 : 1 + steps], refs[1 + steps : 1 + 2 * steps]
-    bands, waves, weights, raw, dense = refs[1 + 2 * steps :]
+def table_kernel(members, terms, shared, taps, half, rows, lines, range_rows, total_range, *refs):
+    packs, bands, waves, weights, raw, dense = refs
     angles = bands.shape[-1]
     member = lax.axis_index("sub") & (members - 1)
     slab = lax.axis_index("rng")
 
     def fill(piece, section):
-        values = piece[...].astype(jnp.float32)
+        values = piece.astype(jnp.float32)
         for term in range(terms):
             weights[section, term] = values[term * taps : (term + 1) * taps]
         start = terms * taps
@@ -108,23 +112,11 @@
         raw[section, 1] = kind[1] + kind[2]
         raw[section, 2] = kind[3] + kind[4] + kind[5]
 
-    if masks:
-        core = slab & 1
-        fill(own, member)
-        for side, received in ((0, mine), (1, theirs)):
-            holder = core if side == 0 else 1 - core
-            for step in range(steps):
-                pair = [masks[c][step] if step < len(masks[c]) else 0 for c in range(2)]
-                mask = jnp.where(holder == 0, pair[0], pair[1])
-
-                @pl.when(mask != 0)
-                def _(step=step, received=received, mask=mask):
-                    fill(received[step], member ^ mask)
-
+    for section in range(members):
+        fill(packs[section] if shared else packs[...], section)
+    if shared:
         first_row, row_step = slab * range_rows + member * rows, 0
     else:
-        for section in range(members):
-            fill(own, section)
         first_row, row_step = slab * range_rows, rows
 
     for start in range(0, members * terms, 8):
@@ -181,7 +173,7 @@
                             jnp.bfloat16
                         )
 
-            if masks:
+            if shared:
                 bands_of()
             else:
                 pl.when(section == 0)(bands_of)
@@ -207,17 +199,16 @@
     lax.fori_loop(0, members * terms, entry, 0)
 
 
-def formed(steering, re_part, im_part):
-    def dot(left, right):
-        return lax.dot_general(
-            left, right, (((1,), (1,)), ((), ())), preferred_element_type=jnp.float32
+def formed(steering, re_parts, im_parts):
+    rows = jnp.concatenate(re_parts + im_parts, axis=0)
+    count = rows.shape[0] // 2
+    by_real, by_imag = [
+        lax.dot_general(
+            rows, steering[c], (((1,), (1,)), ((), ())), preferred_element_type=jnp.float32
         )
-
-    real_weight, imag_weight = steering[0], steering[1]
-    return (
-        dot(re_part, real_weight) + dot(im_part, -imag_weight),
-        dot(re_part, imag_weight) + dot(im_part, real_weight),
-    )
+        for c in range(2)
+    ]
+    return by_real[:count] - by_imag[count:], by_imag[:count] + by_real[count:]
 
 
 def place_of(sub_map, group, slabs, slab, index):
@@ -231,23 +222,30 @@
     return place
 
 
-def form_kernel(group, pulse_count, sources, sub_map, *refs):
+def form_kernel(group, pulse_count, sources, first, count, sub_map, *refs):
     blocks, steering, image = refs[:sources], refs[sources], refs[sources + 1]
     half = image.shape[-1]
     per_source = group // sources
     slab = lax.axis_index("rng")
-
-    def step(piece, carry):
-        columns = pl.ds(pl.multiple_of(piece * pulse_count, pulse_count), pulse_count)
-        for source in range(sources):
-            target = place_of(sub_map, group, sources, slab, source * per_source + piece)
-            parts = [blocks[source][c, :, columns] for c in range(2)]
-            for c, value in enumerate(formed(steering, *parts)):
-                for window in range(2):
-                    image[target, c, window] = value[:, window * half : (window + 1) * half]
-        return carry
-
-    lax.fori_loop(0, per_source, step, 0)
+    for source in range(sources):
+        for start in range(0, per_source, 2):
+            pieces = range(start, min(start + 2, per_source))
+            parts = [
+                [
+                    blocks[source][
+                        c, first : first + count, piece * pulse_count : (piece + 1) * pulse_count
+                    ]
+                    for piece in pieces
+                ]
+                for c in range(2)
+            ]
+            values = formed(steering, *parts)
+            for index, piece in enumerate(pieces):
+                target = place_of(sub_map, group, sources, slab, source * per_source + piece)
+                for c in range(2):
+                    value = values[c][index * count : (index + 1) * count]
+                    for window in range(2):
+                        image[target, c, window] = value[:, window * half : (window + 1) * half]
 
 
 def turned(values, block):
@@ -273,22 +271,21 @@
 
 def merge_kernel(group, segments, rows, pulse_count, sources, sub_map, *refs):
     image, edge, steering, bands, waves = refs[:5]
-    outs, edges = refs[5 : 5 + group], refs[5 + group]
-    stores = refs[6 + group :]
+    outs, edges, stores = refs[5 : 5 + group], refs[5 + group], refs[6 + group :]
     half = image.shape[-1]
     member = lax.axis_index("sub") & (group - 1)
     per_source = group // sources
+
     below = lax.axis_index("rng")
     if sources > 1:
         below = jnp.minimum(below + jnp.where(member == group - 1, 1, 0), sources - 1)
-
-    edge_parts = [[], []]
+    parts = [[], []]
     for source in range(sources):
         for piece in range(per_source):
             columns = slice(piece * pulse_count, (piece + 1) * pulse_count)
             for c in range(2):
-                edge_parts[c].append(edge[source, c, :, columns])
-    values = formed(steering, *[jnp.concatenate(parts, axis=0) for parts in edge_parts])
+                parts[c].append(edge[source, c, :, columns])
+    values = formed(steering, *parts)
     for index in range(group):
         target = place_of(sub_map, group, sources, below, index)
         for c in range(2):
@@ -397,10 +394,8 @@
 
 
 def send_order(group):
-    masks = list(range(1, group))
-    far = sorted([mask for mask in masks if mask >= group // 2], reverse=True)
-    near = sorted([mask for mask in masks if mask < group // 2], reverse=True)
-    return far[:2] + near + far[2:]
+    far, near = list(range(group - 1, group // 2 - 1, -1)), list(range(group // 2 - 1, 0, -1))
+    return far[:1] + near[:-1] + far[1:2] + near[-1:] + far[2:]
 
 
 def on_device(echoes, steering, sub_map, band_offset, interp_weight, range_frac, phase_rate):
@@ -421,7 +416,10 @@
     *quarters, early_pack, late_pack = pl.pallas_call(
         functools.partial(cut_kernel, slabs, segments, taps, half),
         out_shape=[pltpu.VMEM(cut, jnp.bfloat16)] * slabs
-        + [pltpu.VMEM((pack_rows(terms, taps), angles), jnp.bfloat16) for terms in (early, late)],
+        + [
+            pltpu.VMEM((group, pack_rows(early, taps), angles), jnp.bfloat16),
+            pltpu.VMEM((pack_rows(late, taps), angles), jnp.bfloat16),
+        ],
         in_specs=[FAR] * 5,
         out_specs=[WHOLE] * (slabs + 2),
         scratch_shapes=[pltpu.VMEM(value.shape, value.dtype) for value in tables_in]
@@ -435,18 +433,10 @@
     for mask in range(slabs - 1, 0, -1):
         received[mask] = exchanged(quarters[mask], "rng", mask)
 
-    masks = list(range(group - 1, 0, -1))
-    masks = (masks[0::2], masks[1::2])
-    mine, theirs = [], []
-    for step in range(len(masks[0])):
-        route = []
-        for s in range(subs):
-            for q in range(slabs):
-                if step < len(masks[q & 1]):
-                    route.append((s * slabs + q, (s ^ masks[q & 1][step]) * slabs + q))
-        mine.append(lax.ppermute(early_pack, ("sub", "rng"), route))
-    for piece in mine:
-        theirs.append(exchanged(piece, "rng", 1))
+    members = None
+    if groups > 1:
+        members = [[g * group + m for m in range(group)] for g in range(groups)]
+    packs = lax.all_to_all(early_pack, "sub", 0, 0, axis_index_groups=members, tiled=True)
 
     if groups == 1:
         blocks = received
@@ -475,13 +465,13 @@
                 route.append((number * slabs + q, (number + group - 1) * slabs + q - 1))
     edge = lax.ppermute(edge_rows, ("sub", "rng"), route)
 
-    def tables(terms, sources, held, lines, arrays):
+    def tables(terms, shared, held, lines, pack):
         return pl.pallas_call(
             functools.partial(
                 table_kernel,
                 group,
                 terms,
-                sources,
+                shared,
                 taps,
                 half,
                 rows,
@@ -493,7 +483,7 @@
                 jax.ShapeDtypeStruct((held, terms, angles, angles), jnp.bfloat16),
                 jax.ShapeDtypeStruct((group, terms, 2, lines, angles), jnp.float32),
             ),
-            in_specs=[WHOLE] * len(arrays),
+            in_specs=[WHOLE],
             out_specs=(WHOLE, WHOLE),
             scratch_shapes=[
                 pltpu.VMEM((group, terms, taps, angles), jnp.float32),
@@ -502,12 +492,12 @@
             ],
             compiler_params=params(4),
             cost_estimate=cost(2_000_000_000),
-        )(*arrays)
-
-    bands, waves = tables(early, masks, group, rows + 8, [early_pack, *mine, *theirs])
+        )(pack)
+
+    bands, waves = tables(early, True, group, rows + 8, packs)
 
     image = pl.pallas_call(
-        functools.partial(form_kernel, group, pulse_count, len(blocks)),
+        functools.partial(form_kernel, group, pulse_count, len(blocks), 0, rows),
         out_shape=jax.ShapeDtypeStruct((group, 2, 2, rows, half), jnp.float32),
         in_specs=[SCALARS] + [WHOLE] * (len(blocks) + 1),
         out_specs=WHOLE,
@@ -532,16 +522,16 @@
     arrived = {0: sent[0]}
     for mask in order:
         arrived[mask] = exchanged(sent[mask], "sub", mask)
-    last_bands, last_waves = tables(late, None, 1, rows, [late_pack])
+
+    last_bands, last_waves = tables(late, False, 1, rows, late_pack)
     result = None
-    turns = [[0] + order[:1] + order[2:-2], order[1:2], order[-2:-1], order[-1:]]
-    for chosen in turns:
+    turns = [[0] + [mask for mask in order[:-2] if mask != order[3]], [order[3], order[-2]]]
+    for chosen in turns + [order[-1:]]:
         count = len(chosen)
-        shape = jax.ShapeDtypeStruct((2, range_rows, angles), jnp.bfloat16)
         previous = [] if result is None else [result]
         result = pl.pallas_call(
             functools.partial(final_kernel, chosen, group, rows, result is None),
-            out_shape=shape,
+            out_shape=jax.ShapeDtypeStruct((2, range_rows, angles), jnp.bfloat16),
             in_specs=[WHOLE] * (count + 2) + [FAR] * len(previous),
             out_specs=FAR,
             scratch_shapes=[

time: 64.9 us -> 60.6 us (0.934)
  the two profiles are of different devices: /device:TPU:1 before, /device:TPU:7 now
where the time goes in v2:
time: 60.6 us; the launch traced here: 60.3 us
  starting transfers between devices  26.5 us (44%)
  waiting for transfers between devices  18.1 us (30%)
  Pallas kernels  13.8 us (23%)
  local copies, waits for them, and re-layouts  1.66 us (3%)
    ppermute x10, starting transfers between devices, exchanged(): lax.ppermute(block, axis, [(source, source ^ mask) for source in range(co...  18.6 us
    ppermute x10, waiting for transfers between devices, exchanged(): lax.ppermute(block, axis, [(source, source ^ mask) for source in range(co...  18.1 us
    all_to_all x1, starting transfers between devices, on_device(): lax.all_to_all(early_pack, 'sub', 0, 0, axis_index_groups=members, tiled=...  5.78 us
    pallas_call x2, Pallas kernels, tables(): pl.pallas_call(functools.partial(table_kernel, group, terms, shared, taps...  3.98 us
    pallas_call x3, Pallas kernels, on_device(): pl.pallas_call(functools.partial(final_kernel, chosen, group, rows, resul...  3.34 us
    pallas_call x1, Pallas kernels, on_device(): pl.pallas_call(functools.partial(merge_kernel, group, segments, rows, pul...  3.06 us
    ppermute x1, starting transfers between devices, on_device(): edge = lax.ppermute(edge_rows, ('sub', 'rng'), route)  2.16 us
    pallas_call x1, Pallas kernels, on_device(): pl.pallas_call(functools.partial(cut_kernel, slabs, segments, taps, half)...  2.13 us
  transfers between devices with their start and end apart: 12, of which 5 were waited for; matrix products, arithmetic and copies ran while one was open for 0% of the time, Pallas kernels for 13%

profile of v2, /device:TPU:7, one launch (start us, length us, event | category | flops | bytes accessed | tf_op | source)
XLA Modules:
  0.0 60.3 jit_solution(86307437253674181)
XLA Ops:
  0.0 2.1 %cut.1 = (bf16[2,128,512]{2,1,0:T(8,128)(2,1)S(1)}, bf16[2,128,512]{2,1,0:T(8,128)(2,1)S(1)}, bf16[2,128,512]{2,1,0:T(8,128)(2,1)S(1)}, bf16[2,128,512]{2,1,0:T(...) custom-call(bf16[2,4,128,512]{3,2,1,0:T(8,128)(2,1)} %echoes.1, s32[1,3,2,256]{3,2,1,0:T(2,128)} %offset.1, ...), custom_call_target="tpu_custom_call" | custom-call | flops 1000000000 | bytes 1048576 | tf_op jit(solution)/shard_map/cut/pallas_call | solution.py:416
  2.1 0.9 %collective-permute-start.2 = (bf16[2,128,512]{2,1,0:T(8,128)(2,1)S(1)}, bf16[2,128,512]{2,1,0:T(8,128)(2,1)S(1)}, u32[]{:S(2)}, u32[]{:S(2)}) collective-permute-start(bf16[2,128,512]{2,1,0:T(8,128)(2,1)S(1)} %get-tuple-element.26), channel_id=1, source_target_pairs={{0,3},{1,2},{2,1},{3,0},{4,7},{5,6},{6,5},{7,4},{8,11},{9,10},{10,... | collective-permute-start | bytes 786440 | tf_op jit(solution)/shard_map/ppermute | solution.py:21
  3.0 1.2 %collective-permute-start.1 = (bf16[2,128,512]{2,1,0:T(8,128)(2,1)S(1)}, bf16[2,128,512]{2,1,0:T(8,128)(2,1)S(1)}, u32[]{:S(2)}, u32[]{:S(2)}) collective-permute-start(bf16[2,128,512]{2,1,0:T(8,128)(2,1)S(1)} %get-tuple-element.25), channel_id=1, source_target_pairs={{0,2},{1,3},{2,0},{3,1},{4,6},{5,7},{6,4},{7,5},{8,10},{9,11},{10,... | collective-permute-start | bytes 786440 | tf_op jit(solution)/shard_map/ppermute | solution.py:21
  4.2 0.1 collective-permute-start
  4.3 5.8 %all-to-all-start = ((bf16[8,56,256]{2,1,0:T(8,128)(2,1)}), bf16[8,56,256]{2,1,0:T(8,128)(2,1)S(1)}, u32[]{:S(2)}, u32[]{:S(2)}) async-start(bf16[8,56,256]{2,1,0:T(8,128)(2,1)} %get-tuple-element.27), calls=%async_computation | async-start | bytes 458752 | tf_op jit(solution)/shard_map/all_to_all | solution.py:439
  10.1 0.9 %collective-permute-done.2.refs_3_ = bf16[2,128,512]{2,1,0:T(8,128)(2,1)S(1)} collective-permute-done((bf16[2,128,512]{2,1,0:T(8,128)(2,1)S(1)}, bf16[2,128,512]{2,1,0:T(8,128)(2,1)S(1)}, u32[]{:S(2)}, u32[]{:S(2)}) %collective-permute-start.2) | collective-permute-done | bytes 262176 | tf_op jit(solution)/shard_map/ppermute | solution.py:21
  11.1 5.6 %collective-permute-done.1.refs_2_ = bf16[2,128,512]{2,1,0:T(8,128)(2,1)S(1)} collective-permute-done((bf16[2,128,512]{2,1,0:T(8,128)(2,1)S(1)}, bf16[2,128,512]{2,1,0:T(8,128)(2,1)S(1)}, u32[]{:S(2)}, u32[]{:S(2)}) %collective-permute-start.1) | collective-permute-done | bytes 262176 | tf_op jit(solution)/shard_map/ppermute | solution.py:21
  16.7 0.7 %copy-done.1 = bf16[2,128,512]{2,1,0:T(8,128)(2,1)} copy-done((bf16[2,128,512]{2,1,0:T(8,128)(2,1)}, bf16[2,128,512]{2,1,0:T(8,128)(2,1)S(1)}, u32[]{:S(2)}) %copy-start.1) | copy-done | bytes 262168
  17.4 2.2 %collective-permute-start.3 = (bf16[4,2,8,512]{3,2,1,0:T(8,128)(2,1)S(1)}, bf16[4,2,8,512]{3,2,1,0:T(8,128)(2,1)S(1)}, u32[]{:S(2)}, u32[]{:S(2)}) collective-permute-start(bf16[4,2,8,512]{3,2,1,0:T(8,128)(2,1)S(1)} %pad_maximum_fusion), channel_id=1, source_target_pairs={{1,28},{2,29},{3,30},{4,0},{5,1},{6,2},{7,3},{8,4},{9,5},{10,6},{1... | collective-permute-start | bytes 196616 | tf_op jit(solution)/shard_map/ppermute | solution.py:466
  19.6 0.9 %copy-done.2 = bf16[2,128,512]{2,1,0:T(8,128)(2,1)S(1)} copy-done((bf16[2,128,512]{2,1,0:T(8,128)(2,1)S(1)}, bf16[2,128,512]{2,1,0:T(8,128)(2,1)}, u32[]{:S(2)}) %copy-start.2) | copy-done | bytes 262168
  20.6 1.3 %form.1.refs_0_ = f32[8,2,2,128,128]{4,3,2,1,0:T(8,128)S(1)} custom-call(s32[8]{0:T(128)S(1)} %copy-done.3, bf16[2,128,512]{2,1,0:T(8,128)(2,1)S(1)} %get-tuple-element.23.refs_0_, bf16[2,128,512]{2,1,0:T(8,128)(2,1)S(1)} %copy-done.2, bf16[2,128,512]{2,1,0:T(8,128)(2,1)S(1)} %collective-permute-done.1.refs_2_, ...), custom_call_target="tpu_custom_call" | custom-call | flops 1000000000 | bytes 1048576 | tf_op jit(solution)/shard_map/form/pallas_call | solution.py:499
  21.9 2.7 %shard_map.73 = (bf16[8,4,256,256]{3,2,1,0:T(8,128)(2,1)S(1)}, f32[8,4,2,136,256]{4,3,2,1,0:T(8,128)S(1)}) custom-call(bf16[8,56,256]{2,1,0:T(8,128)(2,1)S(1)} %all-to-all-done.refs_0_), custom_call_target="tpu_custom_call" | custom-call | flops 2000000000 | bytes 1048576 | tf_op jit(solution)/shard_map/pallas_call | solution.py:469
  24.6 3.1 %merge.1 = (bf16[520,128]{1,0:T(8,128)(2,1)S(1)}, bf16[520,128]{1,0:T(8,128)(2,1)S(1)}, bf16[520,128]{1,0:T(8,128)(2,1)S(1)}, bf16[520,128]{1,0:T(8,128)(2,1)S(1...) custom-call(s32[8]{0:T(128)S(1)} %copy-done.3, ...), custom_call_target="tpu_custom_call" | custom-call | flops 4000000000 | bytes 1048576 | tf_op jit(solution)/shard_map/merge/pallas_call | solution.py:509
  27.7 4.6 %collective-permute-start.10 = (bf16[520,128]{1,0:T(8,128)(2,1)S(1)}, bf16[520,128]{1,0:T(8,128)(2,1)S(1)}, u32[]{:S(2)}, u32[]{:S(2)}) collective-permute-start(bf16[520,128]{1,0:T(8,128)(2,1)S(1)} %get-tuple-element.40), channel_id=1, source_target_pairs={{0,4},{4,0},{8,12},{12,8},{16,20},{20,16},{24,28},{28,24},{1,5},{5... | collective-permute-start | bytes 399368 | tf_op jit(solution)/shard_map/ppermute | solution.py:21
  32.3 2.2 %collective-permute-start.9 = (bf16[520,128]{1,0:T(8,128)(2,1)S(1)}, bf16[520,128]{1,0:T(8,128)(2,1)S(1)}, u32[]{:S(2)}, u32[]{:S(2)}) collective-permute-start(bf16[520,128]{1,0:T(8,128)(2,1)S(1)} %get-tuple-element.39), channel_id=1, source_target_pairs={{0,8},{4,12},{8,0},{12,4},{16,24},{20,28},{24,16},{28,20},{1,9},{5... | collective-permute-start | bytes 399368 | tf_op jit(solution)/shard_map/ppermute | solution.py:21
  34.5 3.4 %collective-permute-start.5 = (bf16[520,128]{1,0:T(8,128)(2,1)S(1)}, bf16[520,128]{1,0:T(8,128)(2,1)S(1)}, u32[]{:S(2)}, u32[]{:S(2)}) collective-permute-start(bf16[520,128]{1,0:T(8,128)(2,1)S(1)} %get-tuple-element.34), channel_id=1, source_target_pairs={{0,24},{4,28},{8,16},{12,20},{16,8},{20,12},{24,0},{28,4},{1,25},{... | collective-permute-start | bytes 399368 | tf_op jit(solution)/shard_map/ppermute | solution.py:21
  37.9 1.3 %shard_map.74 = (bf16[1,2,256,256]{3,2,1,0:T(8,128)(2,1)S(1)}, f32[8,2,2,128,256]{4,3,2,1,0:T(8,128)S(1)}) custom-call(bf16[32,256]{1,0:T(8,128)(2,1)S(1)} %get-tuple-element.31.refs_0_), custom_call_target="tpu_custom_call" | custom-call | flops 2000000000 | bytes 1048576 | tf_op jit(solution)/shard_map/pallas_call | solution.py:469
  39.2 0.6 %collective-permute-done.7.refs_1_ = bf16[520,128]{1,0:T(8,128)(2,1)S(1)} collective-permute-done((bf16[520,128]{1,0:T(8,128)(2,1)S(1)}, bf16[520,128]{1,0:T(8,128)(2,1)S(1)}, u32[]{:S(2)}, u32[]{:S(2)}) %collective-permute-start.7) | collective-permute-done | bytes 133152 | tf_op jit(solution)/shard_map/ppermute | solution.py:21
  39.9 6.2 %collective-permute-start.4 = (bf16[520,128]{1,0:T(8,128)(2,1)S(1)}, bf16[520,128]{1,0:T(8,128)(2,1)S(1)}, u32[]{:S(2)}, u32[]{:S(2)}) collective-permute-start(bf16[520,128]{1,0:T(8,128)(2,1)S(1)} %get-tuple-element.30), channel_id=1, source_target_pairs={{0,16},{4,20},{8,24},{12,28},{16,0},{20,4},{24,8},{28,12},{1,17},{... | collective-permute-start | bytes 399368 | tf_op jit(solution)/shard_map/ppermute | solution.py:21
  46.0 1.4 %final.3.refs_4_ = bf16[2,1024,256]{2,1,0:T(8,128)(2,1)} custom-call(bf16[520,128]{1,0:T(8,128)(2,1)S(1)} %get-tuple-element.36.refs_0_, bf16[520,128]{1,0:T(8,128)(2,1)S(1)} %collective-permute-done.7.refs_1_, bf16[520,128]{1,0:T(8,128)(2,1)S(1)} %collective-permute-done.8.refs_2_, bf16[520,128]{1,0:T(8,128)(2,1)S(1)} %collective-permute-done.9.refs_3_, ...), custom_call_target="tpu_custom_call" | custom-call | flops 1000000000 | bytes 1048576 | tf_op jit(solution)/shard_map/final/pallas_call | solution.py:532
  47.5 0.1 collective-permute-done.5.refs_0_
  47.6 1.0 %final.4.refs_3_ = bf16[2,1024,256]{2,1,0:T(8,128)(2,1)} custom-call(bf16[520,128]{1,0:T(8,128)(2,1)S(1)} %collective-permute-done.5.refs_0_, bf16[520,128]{1,0:T(8,128)(2,1)S(1)} %collective-permute-done.6.refs_1_, bf16[1,2,256,256]{3,2,1,0:T(8,128)(2,1)S(1)} %get-tuple-element.32.refs_5_.refs_2_.refs_1_, ...), custom_call_target="tpu_custom_call", output_to_operand_aliasing={{}: (4, {})} | custom-call | flops 1000000000 | bytes 1048576 | tf_op jit(solution)/shard_map/final/pallas_call | solution.py:532
  48.6 10.7 %collective-permute-done.4.refs_0_ = bf16[520,128]{1,0:T(8,128)(2,1)S(1)} collective-permute-done((bf16[520,128]{1,0:T(8,128)(2,1)S(1)}, bf16[520,128]{1,0:T(8,128)(2,1)S(1)}, u32[]{:S(2)}, u32[]{:S(2)}) %collective-permute-start.4) | collective-permute-done | bytes 133152 | tf_op jit(solution)/shard_map/ppermute | solution.py:21
  59.4 0.9 %final.5 = bf16[2,1024,256]{2,1,0:T(8,128)(2,1)} custom-call(bf16[520,128]{1,0:T(8,128)(2,1)S(1)} %collective-permute-done.4.refs_0_, bf16[1,2,256,256]{3,2,1,0:T(8,128)(2,1)S(1)} %get-tuple-element.32.refs_5_.refs_2_.refs_1_, f32[8,2,2,128,256]{4,3,2,1,0:T(8,128)S(1)} %get-tuple-element.33.refs_6_.refs_3_.refs_2_, ...), custom_call_target="tpu_custom_call", output_to_operand_aliasing={{}: (3, {})} | custom-call | flops 1000000000 | bytes 1048576 | tf_op jit(solution)/shard_map/final/pallas_call | solution.py:532
  (21 shorter events, 0.1 us)
Async XLA Ops:
  0.0 19.6 %copy-start = (bf16[2,256,256]{2,1,0:T(8,128)(2,1)S(1)}, bf16[2,256,256]{2,1,0:T(8,128)(2,1)}, u32[]{:S(2)}) copy-start(bf16[2,256,256]{2,1,0:T(8,128)(2,1)} %refs_2_.1) | copy-start | bytes 786436
  0.0 19.6 %copy-start.3 = (s32[8]{0:T(128)S(1)}, s32[8]{0:T(128)}, u32[]{:S(2)}) copy-start(s32[8]{0:T(128)} %sub_map.3) | copy-start | bytes 100
  2.1 8.9 %collective-permute-start.2 = (bf16[2,128,512]{2,1,0:T(8,128)(2,1)S(1)}, bf16[2,128,512]{2,1,0:T(8,128)(2,1)S(1)}, u32[]{:S(2)}, u32[]{:S(2)}) collective-permute-start(bf16[2,128,512]{2,1,0:T(8,128)(2,1)S(1)} %get-tuple-element.26), channel_id=1, source_target_pairs={{0,3},{1,2},{2,1},{3,0},{4,7},{5,6},{6,5},{7,4},{8,11},{9,10},{10,... | collective-permute-start | bytes 786440 | tf_op jit(solution)/shard_map/ppermute | solution.py:21
  3.0 13.7 %collective-permute-start.1 = (bf16[2,128,512]{2,1,0:T(8,128)(2,1)S(1)}, bf16[2,128,512]{2,1,0:T(8,128)(2,1)S(1)}, u32[]{:S(2)}, u32[]{:S(2)}) collective-permute-start(bf16[2,128,512]{2,1,0:T(8,128)(2,1)S(1)} %get-tuple-element.25), channel_id=1, source_target_pairs={{0,2},{1,3},{2,0},{3,1},{4,6},{5,7},{6,4},{7,5},{8,10},{9,11},{10,... | collective-permute-start | bytes 786440 | tf_op jit(solution)/shard_map/ppermute | solution.py:21
  4.2 12.5 %collective-permute-start = (bf16[2,128,512]{2,1,0:T(8,128)(2,1)S(1)}, bf16[2,128,512]{2,1,0:T(8,128)(2,1)S(1)}, u32[]{:S(2)}, u32[]{:S(2)}) collective-permute-start(bf16[2,128,512]{2,1,0:T(8,128)(2,1)S(1)} %get-tuple-element.24), channel_id=1, source_target_pairs={{0,1},{1,0},{2,3},{3,2},{4,5},{5,4},{6,7},{7,6},{8,9},{9,8},{10,11... | collective-permute-start | bytes 786440 | tf_op jit(solution)/shard_map/ppermute | solution.py:21
  4.3 17.6 %all-to-all-start = ((bf16[8,56,256]{2,1,0:T(8,128)(2,1)}), bf16[8,56,256]{2,1,0:T(8,128)(2,1)S(1)}, u32[]{:S(2)}, u32[]{:S(2)}) async-start(bf16[8,56,256]{2,1,0:T(8,128)(2,1)} %get-tuple-element.27), calls=%async_computation | async-start | bytes 458752 | tf_op jit(solution)/shard_map/all_to_all | solution.py:439
  16.7 0.7 %copy-start.1 = (bf16[2,128,512]{2,1,0:T(8,128)(2,1)}, bf16[2,128,512]{2,1,0:T(8,128)(2,1)S(1)}, u32[]{:S(2)}) copy-start(bf16[2,128,512]{2,1,0:T(8,128)(2,1)S(1)} %collective-permute-done.refs_1_) | copy-start | bytes 786436
  17.4 7.2 %collective-permute-start.3 = (bf16[4,2,8,512]{3,2,1,0:T(8,128)(2,1)S(1)}, bf16[4,2,8,512]{3,2,1,0:T(8,128)(2,1)S(1)}, u32[]{:S(2)}, u32[]{:S(2)}) collective-permute-start(bf16[4,2,8,512]{3,2,1,0:T(8,128)(2,1)S(1)} %pad_maximum_fusion), channel_id=1, source_target_pairs={{1,28},{2,29},{3,30},{4,0},{5,1},{6,2},{7,3},{8,4},{9,5},{10,6},{1... | collective-permute-start | bytes 196616 | tf_op jit(solution)/shard_map/ppermute | solution.py:466
  19.6 1.0 %copy-start.2 = (bf16[2,128,512]{2,1,0:T(8,128)(2,1)S(1)}, bf16[2,128,512]{2,1,0:T(8,128)(2,1)}, u32[]{:S(2)}) copy-start(bf16[2,128,512]{2,1,0:T(8,128)(2,1)} %copy-done.1) | copy-start | bytes 786436
  27.7 10.2 %collective-permute-start.10 = (bf16[520,128]{1,0:T(8,128)(2,1)S(1)}, bf16[520,128]{1,0:T(8,128)(2,1)S(1)}, u32[]{:S(2)}, u32[]{:S(2)}) collective-permute-start(bf16[520,128]{1,0:T(8,128)(2,1)S(1)} %get-tuple-element.40), channel_id=1, source_target_pairs={{0,4},{4,0},{8,12},{12,8},{16,20},{20,16},{24,28},{28,24},{1,5},{5... | collective-permute-start | bytes 399368 | tf_op jit(solution)/shard_map/ppermute | solution.py:21
  32.3 7.6 %collective-permute-start.7 = (bf16[520,128]{1,0:T(8,128)(2,1)S(1)}, bf16[520,128]{1,0:T(8,128)(2,1)S(1)}, u32[]{:S(2)}, u32[]{:S(2)}) collective-permute-start(bf16[520,128]{1,0:T(8,128)(2,1)S(1)} %get-tuple-element.37), channel_id=1, source_target_pairs={{0,28},{4,24},{8,20},{12,16},{16,12},{20,8},{24,4},{28,0},{1,29},{... | collective-permute-start | bytes 399368 | tf_op jit(solution)/shard_map/ppermute | solution.py:21
  32.3 13.7 %collective-permute-start.8 = (bf16[520,128]{1,0:T(8,128)(2,1)S(1)}, bf16[520,128]{1,0:T(8,128)(2,1)S(1)}, u32[]{:S(2)}, u32[]{:S(2)}) collective-permute-start(bf16[520,128]{1,0:T(8,128)(2,1)S(1)} %get-tuple-element.38), channel_id=1, source_target_pairs={{0,12},{4,8},{8,4},{12,0},{16,28},{20,24},{24,20},{28,16},{1,13},{... | collective-permute-start | bytes 399368 | tf_op jit(solution)/shard_map/ppermute | solution.py:21
  32.3 13.7 %collective-permute-start.9 = (bf16[520,128]{1,0:T(8,128)(2,1)S(1)}, bf16[520,128]{1,0:T(8,128)(2,1)S(1)}, u32[]{:S(2)}, u32[]{:S(2)}) collective-permute-start(bf16[520,128]{1,0:T(8,128)(2,1)S(1)} %get-tuple-element.39), channel_id=1, source_target_pairs={{0,8},{4,12},{8,0},{12,4},{16,24},{20,28},{24,16},{28,20},{1,9},{5... | collective-permute-start | bytes 399368 | tf_op jit(solution)/shard_map/ppermute | solution.py:21
  34.5 13.1 %collective-permute-start.5 = (bf16[520,128]{1,0:T(8,128)(2,1)S(1)}, bf16[520,128]{1,0:T(8,128)(2,1)S(1)}, u32[]{:S(2)}, u32[]{:S(2)}) collective-permute-start(bf16[520,128]{1,0:T(8,128)(2,1)S(1)} %get-tuple-element.34), channel_id=1, source_target_pairs={{0,24},{4,28},{8,16},{12,20},{16,8},{20,12},{24,0},{28,4},{1,25},{... | collective-permute-start | bytes 399368 | tf_op jit(solution)/shard_map/ppermute | solution.py:21
  37.9 9.7 %collective-permute-start.6 = (bf16[520,128]{1,0:T(8,128)(2,1)S(1)}, bf16[520,128]{1,0:T(8,128)(2,1)S(1)}, u32[]{:S(2)}, u32[]{:S(2)}) collective-permute-start(bf16[520,128]{1,0:T(8,128)(2,1)S(1)} %get-tuple-element.35), channel_id=1, source_target_pairs={{0,20},{4,16},{8,28},{12,24},{16,4},{20,0},{24,12},{28,8},{1,21},{... | collective-permute-start | bytes 399368 | tf_op jit(solution)/shard_map/ppermute | solution.py:21
  39.9 19.5 %collective-permute-start.4 = (bf16[520,128]{1,0:T(8,128)(2,1)S(1)}, bf16[520,128]{1,0:T(8,128)(2,1)S(1)}, u32[]{:S(2)}, u32[]{:S(2)}) collective-permute-start(bf16[520,128]{1,0:T(8,128)(2,1)S(1)} %get-tuple-element.30), channel_id=1, source_target_pairs={{0,16},{4,20},{8,24},{12,28},{16,0},{20,4},{24,8},{28,12},{1,17},{... | collective-permute-start | bytes 399368 | tf_op jit(solution)/shard_map/ppermute | solution.py:21
